TPU v7x, 128 devices: a whole 4x4x4 slice. The times are simulated.
128 devices in a mesh: expert: 64 (over z, y, x_lo, core), dp: 2 (over x_hi).
Axes of the slice: x: 4 (x_hi: 2, x_lo: 2; x = x_hi * 2 + x_lo), y: 4, z: 4, core: 2. Of those that a mesh axis runs over, the one named last changes fastest.
Arguments:
- tokens: bfloat16 [16384, 2880], P(('expert', 'dp')), may hold values from -6 to 6
- cotangent: bfloat16 [16384, 2880], P(('expert', 'dp')), may hold values from -3 to 3
- expert_ids: int32 [16384, 4], P(('expert', 'dp')), may hold values from 0 to 63, as said below
- slots: int32 [16384, 4], P(('expert', 'dp')), may hold values from -1 to 5, as said below
- probs: float32 [16384, 4], P(('expert', 'dp')), may hold values from 0.1 to 0.6
- w_gate: bfloat16 [64, 2880, 1440], P('expert', None, 'dp'), may hold values from -0.109375 to 0.109375
- w_up: bfloat16 [64, 2880, 1440], P('expert', None, 'dp'), may hold values from -0.109375 to 0.109375
- w_down: bfloat16 [64, 2880, 1440], P('expert', None, 'dp'), may hold values from -0.15625 to 0.15625
Outputs:
- input_grad: bfloat16 [16384, 2880], P(('expert', 'dp'))
- prob_grad: float32 [16384, 4], P(('expert', 'dp'))
- grad_gate: bfloat16 [64, 2880, 1440], P('expert', None, 'dp')
- grad_up: bfloat16 [64, 2880, 1440], P('expert', None, 'dp')
- grad_down: bfloat16 [64, 2880, 1440], P('expert', None, 'dp')
Inputs may be any that keep to these rules, and one draw needn't show every extreme that they name: `expert_ids`: each row names 4 different experts. Within the 128 tokens of one device, the choices of one expert, taken in order of tokens and then of k, hold 0, 1, 2 and so on up to 5, and -1 after that; in every draw some expert fills all 6 slots from every device.
All inputs are finite; a program needn't handle non-finite values.
Results may differ from a plain program's by a relative error of at most 0.018.
Values may be sent and summed in bfloat16 or wider, within the bound.
No kernel may reach another device: no remote copies, remote signals or barrier semaphores. Data moves between devices by JAX's collectives and lax.ppermute only.
A program may use at most 192 MiB of HBM per device.

v0:
```python
import jax
import jax.numpy as jnp
from jax import lax
from jax.sharding import PartitionSpec as P

ALPHA = 1.702


def split_up(shard, dim, size):
    lengths = shard.shape
    blocks = shard.reshape(*lengths[:dim], size, lengths[dim] // size, *lengths[dim + 1 :])
    return jnp.moveaxis(blocks, dim, 0)


def sum_at_owner(shard, axis, dim):
    blocks = split_up(shard, dim, lax.axis_size(axis))
    arrived = lax.all_to_all(blocks, axis, split_axis=0, concat_axis=0, tiled=True)
    return arrived.astype(jnp.float32).sum(axis=0)


def body(tokens, cotangent, expert_ids, slots, probs, w_gate, w_up, w_down):
    experts = lax.axis_size("expert")
    tok_rows = tokens.shape[0]
    width = tokens.shape[1]
    top_count = expert_ids.shape[1]
    capacity = max(2, 3 * tok_rows * top_count // (4 * experts))
    slot_total = experts * capacity
    kept = slots >= 0
    position = jnp.where(kept, expert_ids * capacity + slots, slot_total)
    owners = jnp.broadcast_to(jnp.arange(tok_rows, dtype=jnp.int32)[:, None], expert_ids.shape)
    slot_owner = (
        jnp.full((slot_total,), -1, jnp.int32)
        .at[position.reshape(-1)]
        .set(owners.reshape(-1), mode="drop")
    )
    slot_prob = (
        jnp.zeros((slot_total,), jnp.float32)
        .at[position.reshape(-1)]
        .set(probs.reshape(-1), mode="drop")
    )
    present = slot_owner >= 0
    source = jnp.maximum(slot_owner, 0)
    lookup = jnp.where(kept, expert_ids * capacity + slots, 0)
    zero_bf = jnp.zeros((), jnp.bfloat16)
    outgoing = jnp.where(present[:, None], tokens[source], zero_bf)
    arrived = lax.all_to_all(
        outgoing.reshape(experts, capacity, width),
        "expert",
        split_axis=0,
        concat_axis=0,
        tiled=True,
    )
    local_rows = arrived.reshape(slot_total, width)
    pair_rows = lax.all_gather(local_rows, "dp", axis=0, tiled=True)
    gate_w = w_gate[0]
    up_w = w_up[0]
    down_w = w_down[0]
    gate_pre = jnp.dot(pair_rows, gate_w, preferred_element_type=jnp.float32)
    up_pre = jnp.dot(pair_rows, up_w, preferred_element_type=jnp.float32)
    sigmoid_val = jax.nn.sigmoid(ALPHA * gate_pre)
    glu_value = gate_pre * sigmoid_val
    hidden = ((up_pre + 1.0) * glu_value).astype(jnp.bfloat16)
    contract_units = (((1,), (1,)), ((), ()))
    contract_rows = (((0,), (0,)), ((), ()))
    own_out = sum_at_owner(
        lax.dot_general(hidden, down_w, contract_units, preferred_element_type=jnp.float32).astype(
            jnp.bfloat16
        ),
        "dp",
        0,
    ).astype(jnp.bfloat16)
    plain_send = jnp.where(present[:, None], cotangent[source], zero_bf)
    plain_rows, prob_rows = (
        lax.all_to_all(
            plain_send.reshape(experts, capacity, width),
            "expert",
            split_axis=0,
            concat_axis=0,
            tiled=True,
        ),
        lax.all_to_all(
            slot_prob.reshape(experts, capacity).astype(jnp.bfloat16),
            "expert",
            split_axis=0,
            concat_axis=0,
            tiled=True,
        ).astype(jnp.float32),
    )
    plain_rows = plain_rows.reshape(slot_total, width)
    prob_rows = prob_rows.reshape(slot_total)
    slot_grad = jnp.einsum("rd,rd->r", plain_rows, own_out, preferred_element_type=jnp.float32)
    weighted = (prob_rows[:, None] * plain_rows.astype(jnp.float32)).astype(jnp.bfloat16)
    pair_cot = lax.all_gather(weighted, "dp", axis=0, tiled=True)
    hidden_grad = jnp.dot(pair_cot, down_w, preferred_element_type=jnp.float32)
    up_grad = (hidden_grad * glu_value).astype(jnp.bfloat16)
    gate_grad = (
        hidden_grad
        * (up_pre + 1.0)
        * (sigmoid_val + ALPHA * gate_pre * sigmoid_val * (1.0 - sigmoid_val))
    ).astype(jnp.bfloat16)
    grad_down = lax.dot_general(
        pair_cot, hidden, contract_rows, preferred_element_type=jnp.float32
    ).astype(jnp.bfloat16)
    grad_gate = lax.dot_general(
        pair_rows, gate_grad, contract_rows, preferred_element_type=jnp.float32
    ).astype(jnp.bfloat16)
    grad_up = lax.dot_general(
        pair_rows, up_grad, contract_rows, preferred_element_type=jnp.float32
    ).astype(jnp.bfloat16)
    result = lax.dot_general(gate_grad, gate_w, contract_units, preferred_element_type=jnp.float32)
    own_input = sum_at_owner(
        (
            result
            + lax.dot_general(up_grad, up_w, contract_units, preferred_element_type=jnp.float32)
        ).astype(jnp.bfloat16),
        "dp",
        0,
    ).astype(jnp.bfloat16)
    back_rows, back_prob = (
        lax.all_to_all(
            own_input.reshape(experts, capacity, width),
            "expert",
            split_axis=0,
            concat_axis=0,
            tiled=True,
        ),
        lax.all_to_all(
            slot_grad.reshape(experts, capacity).astype(jnp.bfloat16),
            "expert",
            split_axis=0,
            concat_axis=0,
            tiled=True,
        ).astype(jnp.float32),
    )
    back_rows = back_rows.reshape(slot_total, width)
    prob_grad = jnp.where(kept, back_prob.reshape(slot_total)[lookup], jnp.float32(0.0))
    picked_grad = back_rows[lookup]
    masked = jnp.where(kept[:, :, None], picked_grad, zero_bf)
    input_grad = jnp.sum(masked, axis=1, dtype=jnp.float32).astype(jnp.bfloat16)
    return (input_grad, prob_grad, grad_gate[None], grad_up[None], grad_down[None])


def solution(mesh):
    return jax.shard_map(
        body,
        mesh=mesh,
        in_specs=(
            P(("expert", "dp"), None),
            P(("expert", "dp"), None),
            P(("expert", "dp"), None),
            P(("expert", "dp"), None),
            P(("expert", "dp"), None),
            P("expert", None, "dp"),
            P("expert", None, "dp"),
            P("expert", None, "dp"),
        ),
        out_specs=(
            P(("expert", "dp"), None),
            P(("expert", "dp"), None),
            P("expert", None, "dp"),
            P("expert", None, "dp"),
            P("expert", None, "dp"),
        ),
        check_vma=False,
    )
```

profile of v0, /device:TPU:1, one launch (start us, length us, event | category | flops | bytes accessed | tf_op | source)
XLA Modules:
  0.0 475.3 jit_solution(521120281229968658)
XLA Ops:
  9.0 2.4 scatter_custom_fusion.1
  11.6 1.5 copy.45
  13.1 1.5 copy.44
  14.5 3.4 gather_fusion
  18.0 4.3 gather.17
  22.3 3.4 gather_fusion.1
  25.7 4.4 gather.19
  30.2 4.2 broadcast_select_fusion
  34.3 50.1 %all_to_all.37 = bf16[64,6,2880]{2,1,0:T(8,128)(2,1)S(1)} all-to-all(bf16[64,6,2880]{2,1,0:T(8,128)(2,1)S(1)} %get-tuple-element.25), channel_id=1, replica_groups=mesh['expert'=64,'dp'=2] {'expert'}, dimensions={0} | all-to-all | bytes 4423680 | tf_op jit(solution)/shard_map/all_to_all | solution.py:46
  84.4 2.6 reshape.124
  87.3 2.4 scatter_custom_fusion
  90.0 12.2 %all_to_all.38 = bf16[64,1,6]{2,1,0:T(2,128)(2,1)S(1)} all-to-all(bf16[64,1,6]{2,1,0:T(2,128)(2,1)S(1)} %convert_element_type.99), channel_id=1, replica_groups=mesh['expert'=64,'dp'=2] {'expert'}, dimensions={0} | all-to-all | bytes 1536 | tf_op jit(solution)/shard_map/all_to_all | solution.py:81
  102.1 5.7 %all-to-all-start.1 = ((bf16[64,6,2880]{2,1,0:T(8,128)(2,1)}), bf16[64,6,2880]{2,1,0:T(8,128)(2,1)}, u32[]{:S(2)}, u32[]{:S(2)}) async-start(bf16[64,6,2880]{2,1,0:T(8,128)(2,1)} %get-tuple-element.26), calls=%async_computation.1 | async-start | bytes 6029312 | tf_op jit(solution)/shard_map/all_to_all | solution.py:74
  108.3 71.5 %all-to-all-done.1 = bf16[64,6,2880]{2,1,0:T(8,128)(2,1)} async-done(((bf16[64,6,2880]{2,1,0:T(8,128)(2,1)}), bf16[64,6,2880]{2,1,0:T(8,128)(2,1)}, u32[]{:S(2)}, u32[]{:S(2)}) %all-to-all-start.1) | async-done | bytes 2211872 | tf_op jit(solution)/shard_map/all_to_all | solution.py:74
  179.8 3.3 reshape.123
  183.1 2.0 multiply_convert_fusion
  185.2 8.6 %fusion.5 = f32[768,720]{0,1:T(8,128)} fusion(bf16[768,2880]{1,0:T(8,128)(2,1)} %all-gather.5.cloned.1.call-done, bf16[1,2880,720]{1,2,0:T(8,128)(2,1)} %param.13), kind=kOutput, calls=%fused_computation.20 | convolution fusion | flops 3185049600 | bytes 10782720 | tf_op jit(solution)/shard_map/dot_general | solution.py:58
  193.8 52.8 %all-gather.3.cloned.1.call-done = bf16[768,2880]{1,0:T(8,128)(2,1)} async-done(((bf16[384,2880]{1,0:T(8,128)(2,1)}), bf16[768,2880]{1,0:T(8,128)(2,1)}) %all-gather.3.cloned.1.call-update) | async-done | bytes 4423696 | tf_op jit(solution)/shard_map/all_gather | solution.py:93
  246.6 6.9 %fusion.11 = f32[768,720]{0,1:T(8,128)S(1)} fusion(bf16[768,2880]{1,0:T(8,128)(2,1)} %all-gather.3.cloned.1.call-done, bf16[1,2880,720]{1,2,0:T(8,128)(2,1)} %param.15), kind=kOutput, calls=%fused_computation.26 | convolution fusion | flops 3185049600 | bytes 10782720 | tf_op jit(solution)/shard_map/dot_general | solution.py:94
  253.6 8.0 %multiply_convert_fusion.1 = (bf16[768,720]{0,1:T(8,128)(2,1)S(1)}, bf16[768,720]{0,1:T(8,128)(2,1)}, bf16[768,720]{0,1:T(8,128)(2,1)}) fusion(f32[768,720]{0,1:T(8,128)S(1)} %copy-done.6, f32[768,720]{0,1:T(8,128)S(1)} %fusion.11, bf16[768,2880]{1,0:T(8,128)(2,1)S(1)} %copy-done.2, bf16[1,2880,720]{1,2,0:T(8,128)(2,1)} %param.14), kind=kOutput, calls=%fused_computation.31 | convolution fusion | flops 3194449920 | bytes 16312320 | tf_op jit(solution)/shard_map/dot_general | solution.py:59
  261.6 4.2 convolution_convert_fusion
  265.8 2.5 copy.65
  268.3 5.9 %all-to-all-start.5 = ((bf16[2,384,2880]{1,2,0:T(8,128)(2,1)}), bf16[2,384,2880]{1,2,0:T(8,128)(2,1)}, u32[]{:S(2)}, u32[]{:S(2)}) async-start(bf16[2,384,2880]{1,2,0:T(8,128)(2,1)} %bitcast.47), calls=%async_computation.5 | async-start | bytes 8847360 | tf_op jit(solution)/shard_map/all_to_all | solution.py:17
  274.2 6.6 %fusion.3 = f32[768,2880]{0,1:T(8,128)S(1)} fusion(bf16[768,720]{0,1:T(8,128)(2,1)} %get-tuple-element.23, bf16[1,2880,720]{1,2,0:T(8,128)(2,1)} %param.13), kind=kOutput, calls=%fused_computation.18 | convolution fusion | flops 3185049600 | bytes 14100480 | tf_op jit(solution)/shard_map/dot_general | solution.py:110
  280.8 6.3 %add_convert_fusion = bf16[768,2880]{0,1:T(8,128)(2,1)S(1)} fusion(f32[768,2880]{0,1:T(8,128)S(1)} %fusion.3, bf16[768,720]{0,1:T(8,128)(2,1)S(1)} %copy-done.3, bf16[1,2880,720]{1,2,0:T(8,128)(2,1)} %param.14), kind=kOutput, calls=%fused_computation.6 | convolution fusion | flops 3189473280 | bytes 18524160 | tf_op jit(solution)/shard_map/dot_general | solution.py:114
  287.1 2.6 copy.66
  289.7 35.1 %all-to-all-done.5 = bf16[2,384,2880]{1,2,0:T(8,128)(2,1)} async-done(((bf16[2,384,2880]{1,2,0:T(8,128)(2,1)}), bf16[2,384,2880]{1,2,0:T(8,128)(2,1)}, u32[]{:S(2)}, u32[]{:S(2)}) %all-to-all-start.5) | async-done | bytes 4423712 | tf_op jit(solution)/shard_map/all_to_all | solution.py:17
  324.8 5.6 %all-to-all-start.3 = ((bf16[2,384,2880]{1,2,0:T(8,128)(2,1)}), bf16[2,384,2880]{1,2,0:T(8,128)(2,1)}, u32[]{:S(2)}, u32[]{:S(2)}) async-start(bf16[2,384,2880]{1,2,0:T(8,128)(2,1)} %bitcast.46), calls=%async_computation.3 | async-start | bytes 8847360 | tf_op jit(solution)/shard_map/all_to_all | solution.py:17
  330.6 3.2 copy.58
  333.8 4.6 reduce_sum.38
  338.4 2.8 multiply_reduce_fusion
  341.2 0.8 convert_element_type.100
  342.0 38.2 %all-to-all-done.3 = bf16[2,384,2880]{1,2,0:T(8,128)(2,1)} async-done(((bf16[2,384,2880]{1,2,0:T(8,128)(2,1)}), bf16[2,384,2880]{1,2,0:T(8,128)(2,1)}, u32[]{:S(2)}, u32[]{:S(2)}) %all-to-all-start.3) | async-done | bytes 4423712 | tf_op jit(solution)/shard_map/all_to_all | solution.py:17
  380.1 10.0 %all-to-all-start.6 = ((bf16[64,1,6]{2,1,0:T(2,128)(2,1)}), bf16[64,1,6]{2,1,0:T(2,128)(2,1)S(1)}, u32[]{:S(2)}, u32[]{:S(2)}) async-start(bf16[64,1,6]{2,1,0:T(2,128)(2,1)} %convert_element_type.100), calls=%async_computation.6 | async-start | bytes 65536 | tf_op jit(solution)/shard_map/all_to_all | solution.py:127
  390.3 5.1 %reduce_sum.36 = bf16[384,2880]{0,1:T(8,128)(2,1)} reduce(bf16[2,384,2880]{1,2,0:T(8,128)(2,1)} %all-to-all-done.3, bf16[]{:T(256)} %constant.13.clone.1), dimensions={0}, to_apply=%region_2.3 | reduce | flops 1105920 | bytes 6635522 | tf_op jit(solution)/shard_map/reduce_sum | solution.py:18
  395.4 2.9 copy.48
  398.3 2.5 reshape.126
  400.8 9.1 %all-to-all-start.4 = ((bf16[64,6,2880]{2,1,0:T(8,128)(2,1)}), bf16[64,6,2880]{2,1,0:T(8,128)(2,1)}, u32[]{:S(2)}, u32[]{:S(2)}) async-start(bf16[64,6,2880]{2,1,0:T(8,128)(2,1)} %reshape.126), calls=%async_computation.4 | async-start | bytes 6029312 | tf_op jit(solution)/shard_map/all_to_all | solution.py:120
  410.0 7.6 %fusion.2 = bf16[1,2880,720]{1,2,0:T(8,128)(2,1)} fusion(bf16[768,720]{0,1:T(8,128)(2,1)S(1)} %copy-done.8, bf16[768,2880]{1,0:T(8,128)(2,1)} %all-gather.3.cloned.1.call-done), kind=kOutput, calls=%fused_computation.17 | convolution fusion | flops 3187123200 | bytes 9676800 | tf_op jit(solution)/shard_map/dot_general | solution.py:101
  417.6 5.1 %fusion = bf16[1,2880,720]{1,2,0:T(8,128)(2,1)} fusion(bf16[768,720]{0,1:T(8,128)(2,1)S(1)} %copy-done.5, bf16[768,2880]{1,0:T(8,128)(2,1)S(1)} %bitcast.53), kind=kOutput, calls=%fused_computation.15 | convolution fusion | flops 3187123200 | bytes 9676800 | tf_op jit(solution)/shard_map/dot_general | solution.py:104
  422.7 5.1 %fusion.1 = bf16[1,2880,720]{1,2,0:T(8,128)(2,1)} fusion(bf16[768,720]{0,1:T(8,128)(2,1)S(1)} %copy-done.4, bf16[768,2880]{1,0:T(8,128)(2,1)S(1)} %bitcast.53), kind=kOutput, calls=%fused_computation.16 | convolution fusion | flops 3187123200 | bytes 9676800 | tf_op jit(solution)/shard_map/dot_general | solution.py:107
  428.1 3.5 gather_fusion.3
  432.3 17.5 %all-to-all-done.4 = bf16[64,6,2880]{2,1,0:T(8,128)(2,1)} async-done(((bf16[64,6,2880]{2,1,0:T(8,128)(2,1)}), bf16[64,6,2880]{2,1,0:T(8,128)(2,1)}, u32[]{:S(2)}, u32[]{:S(2)}) %all-to-all-start.4) | async-done | bytes 2211872 | tf_op jit(solution)/shard_map/all_to_all | solution.py:120
  449.9 3.3 reshape.127
  453.2 3.7 gather_fusion.2
  456.9 4.7 reshape.148
  461.6 4.2 select_reduce_fusion
  465.8 2.3 copy.54
  (60 shorter events, 4.2 us)
Async XLA Ops:
  7.2 178.1 %all-gather.5.cloned.1.call-start = ((), (), s32[]{:S(2)}) async-start(), calls=%async_computation.8 | async-start | bytes 6782976 | tf_op jit(solution)/shard_map/all_gather | solution.py:54
  25.7 4.5 copy-start
  84.4 2.7 copy-start.1
  102.1 77.6 %all-to-all-start.1 = ((bf16[64,6,2880]{2,1,0:T(8,128)(2,1)}), bf16[64,6,2880]{2,1,0:T(8,128)(2,1)}, u32[]{:S(2)}, u32[]{:S(2)}) async-start(bf16[64,6,2880]{2,1,0:T(8,128)(2,1)} %get-tuple-element.26), calls=%async_computation.1 | async-start | bytes 6029312 | tf_op jit(solution)/shard_map/all_to_all | solution.py:74
  107.8 138.7 %all-gather.3.cloned.1.call-start = ((), (), s32[]{:S(2)}) async-start(), calls=%async_computation.7 | async-start | bytes 6782976 | tf_op jit(solution)/shard_map/all_gather | solution.py:93
  246.6 6.9 %copy-start.2 = (bf16[768,2880]{1,0:T(8,128)(2,1)S(1)}, bf16[768,2880]{1,0:T(8,128)(2,1)}, u32[]{:S(2)}) copy-start(bf16[768,2880]{1,0:T(8,128)(2,1)} %all-gather.5.cloned.1.call-done) | copy-start | bytes 13271044
  246.6 6.9 %copy-start.6 = (f32[768,720]{0,1:T(8,128)S(1)}, f32[768,720]{0,1:T(8,128)}, u32[]{:S(2)}) copy-start(f32[768,720]{0,1:T(8,128)} %fusion.5) | copy-start | bytes 6635524
  246.6 14.9 %slice-start.2 = ((s8[4239360]{0:T(1024)(128)(4,1)}), s8[4194304]{0:T(1024)(128)(4,1)S(1)}, s32[]{:S(2)}) async-start(s8[4239360]{0:T(1024)(128)(4,1)} %bitcast.54), calls=%async_computation.11 | async-start | bytes 8388608
  253.6 8.0 %slice-start.3 = ((s8[4239360]{0:T(1024)(128)(4,1)}), s8[45056]{0:T(1024)(128)(4,1)S(1)}, s32[]{:S(2)}) async-start(s8[4239360]{0:T(1024)(128)(4,1)} %bitcast.54), calls=%async_computation.12 | async-start | bytes 90112
  261.5 4.3 copy-start.7
  268.3 56.5 %all-to-all-start.5 = ((bf16[2,384,2880]{1,2,0:T(8,128)(2,1)}), bf16[2,384,2880]{1,2,0:T(8,128)(2,1)}, u32[]{:S(2)}, u32[]{:S(2)}) async-start(bf16[2,384,2880]{1,2,0:T(8,128)(2,1)} %bitcast.47), calls=%async_computation.5 | async-start | bytes 8847360 | tf_op jit(solution)/shard_map/all_to_all | solution.py:17
  274.2 6.6 %copy-start.3 = (bf16[768,720]{0,1:T(8,128)(2,1)S(1)}, bf16[768,720]{0,1:T(8,128)(2,1)}, u32[]{:S(2)}) copy-start(bf16[768,720]{0,1:T(8,128)(2,1)} %get-tuple-element.24) | copy-start | bytes 3317764
  324.8 55.4 %all-to-all-start.3 = ((bf16[2,384,2880]{1,2,0:T(8,128)(2,1)}), bf16[2,384,2880]{1,2,0:T(8,128)(2,1)}, u32[]{:S(2)}, u32[]{:S(2)}) async-start(bf16[2,384,2880]{1,2,0:T(8,128)(2,1)} %bitcast.46), calls=%async_computation.3 | async-start | bytes 8847360 | tf_op jit(solution)/shard_map/all_to_all | solution.py:17
  380.1 20.7 %all-to-all-start.6 = ((bf16[64,1,6]{2,1,0:T(2,128)(2,1)}), bf16[64,1,6]{2,1,0:T(2,128)(2,1)S(1)}, u32[]{:S(2)}, u32[]{:S(2)}) async-start(bf16[64,1,6]{2,1,0:T(2,128)(2,1)} %convert_element_type.100), calls=%async_computation.6 | async-start | bytes 65536 | tf_op jit(solution)/shard_map/all_to_all | solution.py:127
  400.8 9.2 %copy-start.8 = (bf16[768,720]{0,1:T(8,128)(2,1)S(1)}, bf16[768,720]{0,1:T(8,128)(2,1)}, u32[]{:S(2)}) copy-start(bf16[768,720]{0,1:T(8,128)(2,1)} %copy-done.7) | copy-start | bytes 3317764
  400.8 16.7 %slice-start = ((s8[4521984]{0:T(1024)(128)(4,1)}), s8[327680]{0:T(1024)(128)(4,1)S(1)}, s32[]{:S(2)}) async-start(s8[4521984]{0:T(1024)(128)(4,1)} %bitcast.52), calls=%async_computation.9 | async-start | bytes 655360
  400.8 49.0 %all-to-all-start.4 = ((bf16[64,6,2880]{2,1,0:T(8,128)(2,1)}), bf16[64,6,2880]{2,1,0:T(8,128)(2,1)}, u32[]{:S(2)}, u32[]{:S(2)}) async-start(bf16[64,6,2880]{2,1,0:T(8,128)(2,1)} %reshape.126), calls=%async_computation.4 | async-start | bytes 6029312 | tf_op jit(solution)/shard_map/all_to_all | solution.py:120
  410.0 7.6 %slice-start.1 = ((s8[4521984]{0:T(1024)(128)(4,1)}), s8[4194304]{0:T(1024)(128)(4,1)S(1)}, s32[]{:S(2)}) async-start(s8[4521984]{0:T(1024)(128)(4,1)} %bitcast.52), calls=%async_computation.10 | async-start | bytes 8388608
  410.0 7.6 %copy-start.5 = (bf16[768,720]{0,1:T(8,128)(2,1)S(1)}, bf16[768,720]{0,1:T(8,128)(2,1)}, u32[]{:S(2)}) copy-start(bf16[768,720]{0,1:T(8,128)(2,1)} %get-tuple-element.23) | copy-start | bytes 3317764
  417.6 5.1 %copy-start.4 = (bf16[768,720]{0,1:T(8,128)(2,1)S(1)}, bf16[768,720]{0,1:T(8,128)(2,1)}, u32[]{:S(2)}) copy-start(bf16[768,720]{0,1:T(8,128)(2,1)} %get-tuple-element.24) | copy-start | bytes 3317764
Sparse Core Ops, SparseCore 0:
  87.2 93.1 all-gather.4
  185.3 61.2 all-gather.2
where the time goes:
time: 484 us; the launch traced here: 475 us
  waiting for transfers between devices  215 us (44%)
  local copies, waits for them, and re-layouts  63 us (13%)
  blocking collectives  62.3 us (13%)
  matrix products  58.4 us (12%)
  starting transfers between devices  36.6 us (8%)
  other arithmetic  25.1 us (5%)
  between operations  14.8 us (3%)
    all_to_all x2, waiting for transfers between devices, sum_at_owner(): lax.all_to_all(blocks, axis, split_axis=0, concat_axis=0, tiled=True)  73.2 us
    all_to_all x1, waiting for transfers between devices, body(): lax.all_to_all(plain_send.reshape(experts, capacity, width), 'expert', sp...  71.5 us
    all_gather x1, waiting for transfers between devices, body(): pair_cot = lax.all_gather(weighted, 'dp', axis=0, tiled=True)  52.8 us
    all_to_all x1, blocking collectives, body(): lax.all_to_all(outgoing.reshape(experts, capacity, width), 'expert', spli...  50.1 us
    all_to_all x1, waiting for transfers between devices, body(): lax.all_to_all(own_input.reshape(experts, capacity, width), 'expert', spl...  17.5 us
    all_to_all x1, blocking collectives, body(): lax.all_to_all(slot_prob.reshape(experts, capacity).astype(jnp.bfloat16),...  12.2 us
    all_to_all x2, starting transfers between devices, sum_at_owner(): lax.all_to_all(blocks, axis, split_axis=0, concat_axis=0, tiled=True)  11.5 us
    all_to_all x1, starting transfers between devices, body(): lax.all_to_all(slot_grad.reshape(experts, capacity).astype(jnp.bfloat16),...  9.98 us
  transfers between devices with their start and end apart: 7, of which 5 were waited for; matrix products, arithmetic and copies ran while one was open for 16% of the time, Pallas kernels for 0%

commit v1 on v0

v1 whole, which is shorter than its diff:
```python
import functools

import jax
import jax.numpy as jnp
from jax import lax
from jax.experimental import pallas as pl
from jax.experimental.pallas import tpu as pltpu
from jax.sharding import PartitionSpec as P


ALPHA = 1.702
CHUNKS = 4
GROUP = 8
HALVES = 2
PIECES = 4
BF = jnp.bfloat16
F32 = jnp.float32
NT = (((1,), (1,)), ((), ()))
NN = (((1,), (0,)), ((), ()))
TN = (((0,), (0,)), ((), ()))
ANY = pl.BlockSpec(memory_space=pl.ANY)
VMEM = pl.BlockSpec(memory_space=pltpu.VMEM)
PARAMS = pltpu.CompilerParams(vmem_limit_bytes=60 * 1024 * 1024)


def unpermute_group(recv, pick, rows_ref, b, part, width):
    size = pick.shape[0]
    lane_rows = size // CHUNKS
    blk = recv[pl.ds(pl.multiple_of(b * size, size), size), :]
    out = lax.dot_general(pick, blk, NN, preferred_element_type=F32).astype(BF)
    at = pl.ds(pl.multiple_of(b * lane_rows, lane_rows), lane_rows)
    for c in range(CHUNKS):
        w = min(part, width - c * part)
        rows_ref[at, c * part : c * part + w] = out[c * lane_rows : (c + 1) * lane_rows, :w]


def gate_up_kernel(part, recv, order, wg, wu, rows_ref, hidden, glu, slope):
    width = wg.shape[1]
    m = rows_ref.shape[0] // HALVES
    pick = order[...]

    def sort(b, carry):
        unpermute_group(recv, pick, rows_ref, b, part, width)
        return carry

    lax.fori_loop(0, recv.shape[0] // order.shape[0], sort, 0, unroll=2)

    def step(i, carry):
        at = pl.ds(pl.multiple_of(i * m, m), m)
        rows = rows_ref[at, :]
        g = lax.dot_general(rows, wg[...], NT, preferred_element_type=F32)
        u = lax.dot_general(rows, wu[...], NT, preferred_element_type=F32) + 1.0
        s = jax.nn.sigmoid(ALPHA * g)
        gl = g * s
        hidden[at, :] = (u * gl).astype(BF)
        glu[at, :] = gl
        slope[at, :] = u * (s + ALPHA * g * s * (1.0 - s))
        return carry

    lax.fori_loop(0, HALVES, step, 0)


def gate_up(recv, order, wg, wu):
    units, width = wg.shape
    total, part = recv.shape[0] // CHUNKS, recv.shape[1]
    like = jax.ShapeDtypeStruct
    return pl.pallas_call(
        functools.partial(gate_up_kernel, part),
        out_shape=(
            like((total, width), BF),
            like((total, units), BF),
            like((total, units), F32),
            like((total, units), F32),
        ),
        in_specs=[VMEM] * 4,
        out_specs=(VMEM,) * 4,
        compiler_params=PARAMS,
        name="gate_up",
    )(recv, order, wg, wu)


def row_back_kernel(
    part, recv_hbm, order, order_t, wd_hbm, wg_hbm, wu_hbm, hidden_hbm, glu_hbm, slope_hbm,
    ret_hbm, rows_hbm, gate_hbm, up_hbm,
    recv, wd, wg, wu, hidden, glu, slope, rows, gate_grad, up_grad, wide, in_sems, piece_sems, out_sems,
):
    width = wg.shape[1]
    total = rows.shape[0]
    m = total // HALVES
    last = width - (CHUNKS - 1) * part
    mark = -(-last // 128) * 128
    size = order.shape[0]
    lane_rows = size // CHUNKS
    groups = recv.shape[0] // size
    span = recv.shape[0] // PIECES

    def piece(p):
        at = pl.ds(p * span, span)
        return pltpu.make_async_copy(recv_hbm.at[at], recv.at[at], piece_sems.at[p])

    pairs = [(wd_hbm, wd), (hidden_hbm, hidden), (glu_hbm, glu), (slope_hbm, slope), (wg_hbm, wg), (wu_hbm, wu)]
    loads = [pltpu.make_async_copy(src, dst, in_sems.at[i]) for i, (src, dst) in enumerate(pairs)]
    for p in range(PIECES):
        piece(p).start()
    for load in loads:
        load.start()
    pick = order[...]
    for p in range(PIECES):
        piece(p).wait()

        def step(b, carry):
            unpermute_group(recv, pick, rows, b, part, width)
            return carry

        lax.fori_loop(p * groups // PIECES, (p + 1) * groups // PIECES, step, 0, unroll=2)
    stores = [pltpu.make_async_copy(rows, rows_hbm, out_sems.at[0])]
    stores[0].start()
    pick_t = order_t[...]
    for i in range(HALVES):
        at = pl.ds(i * m, m)
        if i == 0:
            loads[0].wait()
        hg = lax.dot_general(rows[at, :], wd[...], NT, preferred_element_type=F32)
        if i == 0:
            for load in loads[1:4]:
                load.wait()
        sg = jnp.sum(hg * hidden[at, :].astype(F32), axis=1, keepdims=True)
        ug = (hg * glu[at, :]).astype(BF)
        gg = (hg * slope[at, :]).astype(BF)
        gate_grad[at, :] = gg
        up_grad[at, :] = ug
        for j, (src, dst) in enumerate(((gate_grad, gate_hbm), (up_grad, up_hbm))):
            stores.append(pltpu.make_async_copy(src.at[at], dst.at[at], out_sems.at[1 + 3 * i + j]))
            stores[-1].start()
        low = sg - sg.astype(BF).astype(F32)
        lane = lax.broadcasted_iota(jnp.int32, (m, part - mark), 1)
        tail = jnp.where(lane == 0, sg, jnp.where(lane == 1, low, 0.0)).astype(BF)
        if last < mark:
            wide[CHUNKS - 1, :, mark - 128 : mark] = jnp.zeros((m, 128), BF)
        wide[CHUNKS - 1, :, mark:] = tail
        if i == 0:
            for load in loads[4:]:
                load.wait()
        for c in range(CHUNKS):
            w = min(part, width - c * part)
            x = lax.dot_general(gg, wg[:, c * part : c * part + w], NN, preferred_element_type=F32)
            x = x + lax.dot_general(ug, wu[:, c * part : c * part + w], NN, preferred_element_type=F32)
            wide[c, :, :w] = x.astype(BF)

        def put(b, carry):
            src = pl.ds(pl.multiple_of(b * lane_rows, lane_rows), lane_rows)
            blk = jnp.concatenate([wide[c, src, :] for c in range(CHUNKS)], axis=0)
            out = lax.dot_general(pick_t, blk, NN, preferred_element_type=F32)
            dst = pl.ds(pl.multiple_of(i * (groups // HALVES) * size + b * size, size), size)
            recv[dst, :] = out.astype(BF)
            return carry

        lax.fori_loop(0, groups // HALVES, put, 0, unroll=2)
        half = pl.ds(i * (recv.shape[0] // HALVES), recv.shape[0] // HALVES)
        stores.append(pltpu.make_async_copy(recv.at[half], ret_hbm.at[half], out_sems.at[3 + 3 * i]))
        stores[-1].start()
    for store in stores:
        store.wait()


def row_back(recv, order, order_t, wd, wg, wu, hidden, glu, slope):
    units, width = wg.shape
    total, part = recv.shape[0] // CHUNKS, recv.shape[1]
    like = jax.ShapeDtypeStruct
    return pl.pallas_call(
        functools.partial(row_back_kernel, part),
        out_shape=(like(recv.shape, BF), like((total, width), BF), like((total, units), BF), like((total, units), BF)),
        in_specs=[ANY, VMEM, VMEM] + [ANY] * 6,
        out_specs=(ANY,) * 4,
        scratch_shapes=[
            pltpu.VMEM(recv.shape, BF),
            pltpu.VMEM((units, width), BF),
            pltpu.VMEM((units, width), BF),
            pltpu.VMEM((units, width), BF),
            pltpu.VMEM((total, units), BF),
            pltpu.VMEM((total, units), F32),
            pltpu.VMEM((total, units), F32),
            pltpu.VMEM((total, width), BF),
            pltpu.VMEM((total, units), BF),
            pltpu.VMEM((total, units), BF),
            pltpu.VMEM((CHUNKS, total // HALVES, part), BF),
            pltpu.SemaphoreType.DMA((6,)),
            pltpu.SemaphoreType.DMA((PIECES,)),
            pltpu.SemaphoreType.DMA((1 + 3 * HALVES,)),
        ],
        compiler_params=PARAMS,
        name="row_back",
    )(recv, order, order_t, wd, wg, wu, hidden, glu, slope)


def combine_kernel(part, width, back, hits, masks, probs, input_grad, prob_grad, acc, pacc):
    step = pl.program_id(0)
    tops, tok = probs.shape
    last = width - (CHUNKS - 1) * part
    mark = -(-last // 128) * 128

    @pl.when(step == 0)
    def _():
        acc[...] = jnp.zeros_like(acc)
        pacc[...] = jnp.zeros_like(pacc)

    hit = hits[...]
    own = hit[:tok]
    for k in range(1, tops):
        own = own + hit[k * tok : (k + 1) * tok]
    mask = masks[...]
    spread = jnp.concatenate([own * mask[c : c + 1] for c in range(CHUNKS)], axis=0)
    blk = back[...]
    acc[...] += lax.dot_general(spread, blk, NN, preferred_element_type=F32)
    pacc[...] += lax.dot_general(hit * mask[CHUNKS - 1 : CHUNKS], blk[:, mark : mark + 128], NN, preferred_element_type=F32)

    @pl.when(step == pl.num_programs(0) - 1)
    def _():
        for c in range(CHUNKS):
            w = min(part, width - c * part)
            input_grad[c * part : c * part + w, :] = acc[c * tok : (c + 1) * tok, :].T[:w].astype(BF)
        for k in range(tops):
            col = pacc[k * tok : (k + 1) * tok, :].T
            prob_grad[k : k + 1, :] = (col[0:1] + col[1:2]) / probs[k : k + 1, :]


def combine(back, hits, masks, probs_t, width):
    rows, part = back.shape
    tops, tok = probs_t.shape
    span = masks.shape[1]
    turns = hits.shape[1] // span
    like = jax.ShapeDtypeStruct
    return pl.pallas_call(
        functools.partial(combine_kernel, part, width),
        grid=(rows // span,),
        out_shape=(like((width, tok), BF), like((tops, tok), F32)),
        in_specs=[
            pl.BlockSpec((span, part), lambda i: (i, 0)),
            pl.BlockSpec((tops * tok, span), lambda i: (0, i % turns)),
            pl.BlockSpec((CHUNKS, span), lambda i: (0, 0)),
            pl.BlockSpec((tops, tok), lambda i: (0, 0)),
        ],
        out_specs=(pl.BlockSpec((width, tok), lambda i: (0, 0)), pl.BlockSpec((tops, tok), lambda i: (0, 0))),
        scratch_shapes=[pltpu.VMEM((CHUNKS * tok, part), F32), pltpu.VMEM((tops * tok, 128), F32)],
        compiler_params=pltpu.CompilerParams(vmem_limit_bytes=24 * 1024 * 1024),
        name="combine",
    )(back, hits, masks, probs_t)


def divide(x, by):
    return jnp.floor((x.astype(F32) + 0.5) * (1.0 / by)).astype(jnp.int32)


def build_kernel(weigh, part, capacity, rows_t, position, probs, out, wide):
    width, tok = rows_t.shape
    tops = position.shape[0]

    @pl.when(pl.program_id(0) == 0)
    def _():
        wide[:width] = rows_t[...]
        wide[width:] = jnp.zeros((wide.shape[0] - width, tok), BF)

    n = out.shape[1]
    row = pl.program_id(0) * n + lax.broadcasted_iota(jnp.int32, (n, 1), 0)
    expert = divide(row, CHUNKS * capacity)
    row = row - expert * (CHUNKS * capacity)
    chunk = divide(row, capacity)
    slot = expert * capacity + row - chunk * capacity
    own = jnp.zeros((n, tok), F32)
    prob = jnp.zeros((n, tok), F32)
    for k in range(tops):
        hit = slot == position[k : k + 1, :]
        own = jnp.where(hit, 1.0, own)
        prob = jnp.where(hit, probs[k : k + 1, :], prob)
    total = jnp.zeros((n, part), F32)
    for c in range(CHUNKS):
        pick = jnp.where(chunk == c, own, 0.0).astype(BF)
        total = total + lax.dot_general(pick, wide[c * part : (c + 1) * part, :], NT, preferred_element_type=F32)
    if weigh:
        total = total * jnp.sum(prob, axis=1, keepdims=True)
    total = total.astype(BF)
    for d in range(out.shape[0]):
        out[d] = total


def build(weigh, rows_t, position, probs, capacity, rows, part, holders):
    width, tok = rows_t.shape
    tops = position.shape[0]
    span = rows // 4
    whole = lambda shape: pl.BlockSpec(shape, lambda i: (0,) * len(shape))
    return pl.pallas_call(
        functools.partial(build_kernel, weigh, part, capacity),
        grid=(rows // span,),
        out_shape=jax.ShapeDtypeStruct((holders, rows, part), BF),
        in_specs=[whole((width, tok)), whole((tops, tok)), whole((tops, tok))],
        out_specs=pl.BlockSpec((holders, span, part), lambda i: (0, i, 0)),
        scratch_shapes=[pltpu.VMEM((CHUNKS * part, tok), BF)],
        compiler_params=PARAMS,
        name="build_weighted" if weigh else "build_rows",
    )(rows_t, position, probs)


def body(tokens, cotangent, expert_ids, slots, probs, w_gate, w_up, w_down):
    experts = lax.axis_size("expert")
    holders = lax.axis_size("dp")
    tok_rows, width = tokens.shape
    top_count = expert_ids.shape[1]
    capacity = max(2, 3 * tok_rows * top_count // (4 * experts))
    part = -(-width // (CHUNKS * 128)) * 128
    devices = holders * experts
    block = CHUNKS * capacity
    send_rows = experts * block
    position = jnp.where(slots >= 0, expert_ids * capacity + slots, -1).T
    probs_t = probs.T

    row = jnp.arange(send_rows, dtype=jnp.int32)
    row_slot = (row // block) * capacity + row % capacity
    row_chunk = (row // capacity) % CHUNKS

    i = jnp.arange(GROUP * block, dtype=jnp.int32)
    source, chunk, slot = (i // capacity) % GROUP, i // (GROUP * capacity), i % capacity
    target = source * block + chunk * capacity + slot
    order = (target[:, None] == i[None, :]).astype(BF)
    order_t = (i[:, None] == target[None, :]).astype(BF)

    def exchange(blocks):
        blocks = blocks.reshape(devices, block, part)
        blocks = lax.all_to_all(blocks, ("dp", "expert"), split_axis=0, concat_axis=0, tiled=True)
        return blocks.reshape(devices * block, part)

    gate_w = w_gate[0].T
    up_w = w_up[0].T
    down_w = w_down[0].T
    place = (position, probs_t, capacity, send_rows, part, holders)
    token_half = build(False, tokens.T, *place)
    cot_half = build(True, cotangent.T, *place)
    token_recv = exchange(token_half)
    hits = (position.reshape(top_count * tok_rows, 1) == row_slot[None, :]).astype(BF)
    masks = (row_chunk[None, : send_rows // 4] == jnp.arange(CHUNKS)[:, None]).astype(BF)
    cot_half, token_recv = lax.optimization_barrier((cot_half, token_recv))
    cot_recv = exchange(cot_half)
    rows, hidden, glu, slope = gate_up(token_recv, order, gate_w, up_w)
    ret, weighted, gate_grad, up_grad = row_back(
        cot_recv, order, order_t, down_w, gate_w, up_w, hidden, glu, slope
    )
    back = exchange(ret)
    grad_down = lax.dot_general(weighted, hidden, TN, preferred_element_type=F32).astype(BF)
    grad_gate = lax.dot_general(rows, gate_grad, TN, preferred_element_type=F32).astype(BF)
    grad_up = lax.dot_general(rows, up_grad, TN, preferred_element_type=F32).astype(BF)
    input_grad, prob_grad = combine(back, hits, masks, probs_t, width)
    return (input_grad.T, prob_grad.T, grad_gate[None], grad_up[None], grad_down[None])


def solution(mesh):
    tokens = P(("expert", "dp"), None)
    weights = P("expert", None, "dp")
    return jax.shard_map(
        body,
        mesh=mesh,
        in_specs=(tokens,) * 5 + (weights,) * 3,
        out_specs=(tokens,) * 2 + (weights,) * 3,
        check_vma=False,
    )
```

time: 484 us -> 246 us (0.51); the launches traced: 475 us -> 245 us
  waiting for transfers between devices: 215 us -> 130 us
  Pallas kernels: 0 us -> 63.6 us
  local copies, waits for them, and re-layouts: 63 us -> 0.03 us
  blocking collectives: 62.3 us -> 0 us
  matrix products: 58.4 us -> 18.3 us
  other arithmetic: 25.1 us -> 2.41 us
  between operations: 14.8 us -> 0.77 us
  starting transfers between devices: 36.6 us -> 29.2 us
    pallas_call x0 -> x5, Pallas kernels: none -> 63.6 us  [the longest x1 24.5 us: row_back(): pl.pallas_call(functools.partial(row_back_kernel, part), out_shape=(like(...]
    all_to_all x2 -> x0, blocking collectives: 62.3 us -> none  [the longest x1 50.1 us: body(): lax.all_to_all(outgoing.reshape(experts, capacity, width), 'expert', spli...]
    all_gather x2 -> x0, waiting for transfers between devices: 52.8 us -> none  [the longest x1 52.8 us: body(): pair_cot = lax.all_gather(weighted, 'dp', axis=0, tiled=True)]
    dot_general x9 -> x3, matrix products: 58.4 us -> 18.3 us  [the longest x1 7.88 us: body(): lax.dot_general(weighted, hidden, TN, preferred_element_type=F32).astype(BF)]
    all_to_all x5 -> x3, waiting for transfers between devices: 162 us -> 130 us  [exchange(): lax.all_to_all(blocks, ('dp', 'expert'), split_axis=0, concat_axis=0, til...]
    gather x9 -> x0, local copies, waits for them, and re-layouts: 27.7 us -> none  [the longest x2 8.38 us: body(): picked_grad = back_rows[lookup]]
    reshape x9 -> x0, local copies, waits for them, and re-layouts: 17.2 us -> none  [the longest x2 5.05 us: split_up(): shard.reshape(*lengths[:dim], size, lengths[dim] // size, *lengths[dim +...]
    reduce_sum x3 -> x0, other arithmetic: 13.9 us -> none  [the longest x2 9.66 us: sum_at_owner(): return arrived.astype(jnp.float32).sum(axis=0)]
  transfers between devices with their start and end apart: 7 -> 3, of which waited for: 5 -> 3; matrix products, arithmetic and copies ran while one was open for 16% -> 8% of each run, Pallas kernels for 0% -> 10%
where the time goes in v1:
time: 246 us; the launch traced here: 245 us
  waiting for transfers between devices  130 us (53%)
  Pallas kernels  63.6 us (26%)
  starting transfers between devices  29.2 us (12%)
  matrix products  18.3 us (7%)
    all_to_all x3, waiting for transfers between devices, exchange(): lax.all_to_all(blocks, ('dp', 'expert'), split_axis=0, concat_axis=0, til...  130 us
    all_to_all x3, starting transfers between devices, exchange(): lax.all_to_all(blocks, ('dp', 'expert'), split_axis=0, concat_axis=0, til...  29.2 us
    pallas_call x1, Pallas kernels, row_back(): pl.pallas_call(functools.partial(row_back_kernel, part), out_shape=(like(...  24.5 us
    pallas_call x1, Pallas kernels, gate_up(): pl.pallas_call(functools.partial(gate_up_kernel, part), out_shape=(like((...  18.1 us
    pallas_call x2, Pallas kernels, build(): pl.pallas_call(functools.partial(build_kernel, weigh, part, capacity), gr...  11.9 us
    pallas_call x1, Pallas kernels, combine(): pl.pallas_call(functools.partial(combine_kernel, part, width), grid=(rows...  9.13 us
    dot_general x1, matrix products, body(): lax.dot_general(weighted, hidden, TN, preferred_element_type=F32).astype(BF)  7.88 us
    dot_general x1, matrix products, body(): lax.dot_general(rows, gate_grad, TN, preferred_element_type=F32).astype(BF)  5.23 us
  transfers between devices with their start and end apart: 3, of which 3 were waited for; matrix products, arithmetic and copies ran while one was open for 8% of the time, Pallas kernels for 10%

profile of v1, /device:TPU:1, one launch (start us, length us, event | category | flops | bytes accessed | tf_op | source)
XLA Modules:
  0.0 244.6 jit_solution(10281563056779293771)
XLA Ops:
  0.6 1.3 fusion.25
  1.9 5.9 %build_rows.1 = bf16[2,1536,768]{2,1,0:T(8,128)(2,1)} custom-call(bf16[2880,128]{1,0:T(8,128)(2,1)} %bitcast.48, s32[4,128]{1,0:T(4,128)} %get-tuple-element.30.position, f32[4,128]{1,0:T(4,128)} %bitcast.37), custom_call_target="tpu_custom_call" | custom-call | tf_op jit(solution)/shard_map/build_rows/pallas_call | solution.py:291
  7.8 11.9 %all-to-all-start = ((bf16[128,24,768]{2,1,0:T(8,128)(2,1)}), bf16[128,24,768]{2,1,0:T(8,128)(2,1)}, u32[]{:S(2)}, u32[]{:S(2)}) async-start(bf16[128,24,768]{2,1,0:T(8,128)(2,1)} %bitcast.41), calls=%async_computation | async-start | bytes 9437184 | tf_op jit(solution)/shard_map/all_to_all | solution.py:328
  19.7 5.9 %build_weighted.1 = bf16[2,1536,768]{2,1,0:T(8,128)(2,1)} custom-call(bf16[2880,128]{1,0:T(8,128)(2,1)} %bitcast.49, s32[4,128]{1,0:T(4,128)} %get-tuple-element.30.position, f32[4,128]{1,0:T(4,128)} %bitcast.38), custom_call_target="tpu_custom_call" | custom-call | tf_op jit(solution)/shard_map/build_weighted/pallas_call | solution.py:291
  25.7 52.0 %all-to-all-done = bf16[128,24,768]{2,1,0:T(8,128)(2,1)} async-done(((bf16[128,24,768]{2,1,0:T(8,128)(2,1)}), bf16[128,24,768]{2,1,0:T(8,128)(2,1)}, u32[]{:S(2)}, u32[]{:S(2)}) %all-to-all-start) | async-done | bytes 4718624 | tf_op jit(solution)/shard_map/all_to_all | solution.py:328
  77.7 8.6 %all-to-all-start.1 = ((bf16[128,24,768]{2,1,0:T(8,128)(2,1)}), bf16[128,24,768]{2,1,0:T(8,128)(2,1)}, u32[]{:S(2)}, u32[]{:S(2)}) async-start(bf16[128,24,768]{2,1,0:T(8,128)(2,1)} %bitcast.40), calls=%async_computation.1 | async-start | bytes 9437184 | tf_op jit(solution)/shard_map/all_to_all | solution.py:328
  86.3 0.7 fusion.4
  87.0 18.1 %gate_up.1 = (bf16[768,2880]{1,0:T(8,128)(2,1)}, bf16[768,720]{1,0:T(8,128)(2,1)}, f32[768,720]{1,0:T(8,128)}, f32[768,720]{1,0:T(8,128)}) custom-call(bf16[3072,768]{1,0:T(8,128)(2,1)} %bitcast.5.recv, bf16[192,192]{1,0:T(8,128)(2,1)} %get-tuple-element.32.order, bf16[720,2880]{1,0:T(8,128)(2,1)} %bitcast.42, bf16[720,2880]{1,0:T(8,128)(2,1)} %bitcast.44), custom_call_target="tpu_custom_call" | custom-call | tf_op jit(solution)/shard_map/gate_up/pallas_call | solution.py:67
  105.1 39.1 %all-to-all-done.1 = bf16[128,24,768]{2,1,0:T(8,128)(2,1)} async-done(((bf16[128,24,768]{2,1,0:T(8,128)(2,1)}), bf16[128,24,768]{2,1,0:T(8,128)(2,1)}, u32[]{:S(2)}, u32[]{:S(2)}) %all-to-all-start.1) | async-done | bytes 4718624 | tf_op jit(solution)/shard_map/all_to_all | solution.py:328
  144.2 24.5 %row_back.1 = (bf16[3072,768]{1,0:T(8,128)(2,1)}, bf16[768,2880]{1,0:T(8,128)(2,1)}, bf16[768,720]{1,0:T(8,128)(2,1)}, bf16[768,720]{1,0:T(8,128)(2,1)}) custom-call(bf16[3072,768]{1,0:T(8,128)(2,1)} %bitcast.7.recv_hbm, bf16[192,192]{1,0:T(8,128)(2,1)} %get-tuple-element.32.order, bf16[192,192]{1,0:T(8,128)(2,1)} %get-tuple-element.31.order_t, ...), custom_call_target="tpu_custom_call" | custom-call | tf_op jit(solution)/shard_map/row_back/pallas_call | solution.py:170
  168.8 0.0 copy-start.1
  168.8 8.7 %all-to-all-start.2 = ((bf16[128,24,768]{2,1,0:T(8,128)(2,1)}), bf16[128,24,768]{2,1,0:T(8,128)(2,1)}, u32[]{:S(2)}, u32[]{:S(2)}) async-start(bf16[128,24,768]{2,1,0:T(8,128)(2,1)} %bitcast.46), calls=%async_computation.2 | async-start | bytes 9437184 | tf_op jit(solution)/shard_map/all_to_all | solution.py:328
  177.6 0.0 slice-start
  177.6 0.3 compare_convert_fusion.hits
  177.9 0.0 copy-done.1
  177.9 0.0 slice-start.1
  177.9 0.0 copy-start.3
  177.9 7.9 %fusion.2 = bf16[1,2880,720]{1,2,0:T(8,128)(2,1)} fusion(bf16[768,2880]{1,0:T(8,128)(2,1)} %get-tuple-element.28, bf16[768,720]{1,0:T(8,128)(2,1)S(1)} %copy-done.1), kind=kOutput, calls=%fused_computation.5 | convolution fusion | flops 3187123200 | bytes 9676800 | tf_op jit(solution)/shard_map/dot_general | solution.py:347
  185.8 0.0 slice-done
  185.8 0.0 slice-done.1
  185.8 0.0 copy-done.3
  185.8 0.0 copy-start.2
  185.9 5.2 %fusion.1 = bf16[1,2880,720]{1,2,0:T(8,128)(2,1)} fusion(bf16[768,2880]{1,0:T(8,128)(2,1)S(1)} %bitcast.51, bf16[768,720]{1,0:T(8,128)(2,1)S(1)} %copy-done.3), kind=kOutput, calls=%fused_computation.4 | convolution fusion | flops 3187123200 | bytes 9676800 | tf_op jit(solution)/shard_map/dot_general | solution.py:349
  191.1 0.0 copy-done.2
  191.1 0.0 copy-start
  191.1 5.2 %fusion = bf16[1,2880,720]{1,2,0:T(8,128)(2,1)} fusion(bf16[768,2880]{1,0:T(8,128)(2,1)S(1)} %bitcast.51, bf16[768,720]{1,0:T(8,128)(2,1)S(1)} %copy-done.2), kind=kOutput, calls=%fused_computation.3 | convolution fusion | flops 3187123200 | bytes 9676800 | tf_op jit(solution)/shard_map/dot_general | solution.py:348
  196.3 39.1 %all-to-all-done.2 = bf16[128,24,768]{2,1,0:T(8,128)(2,1)} async-done(((bf16[128,24,768]{2,1,0:T(8,128)(2,1)}), bf16[128,24,768]{2,1,0:T(8,128)(2,1)}, u32[]{:S(2)}, u32[]{:S(2)}) %all-to-all-start.2) | async-done | bytes 4718624 | tf_op jit(solution)/shard_map/all_to_all | solution.py:328
  235.5 0.0 copy-done
  235.5 9.1 %combine.1 = (bf16[2880,128]{1,0:T(8,128)(2,1)}, f32[4,128]{1,0:T(4,128)}) custom-call(bf16[3072,768]{1,0:T(8,128)(2,1)} %bitcast.17.back, bf16[512,1536]{1,0:T(8,128)(2,1)S(1)} %compare_convert_fusion.hits, bf16[4,384]{1,0:T(4,128)(2,1)S(1)} %fusion.16.masks, f32[4,128]{1,0:T(4,128)S(1)} %bitcast.39), custom_call_target="tpu_custom_call" | custom-call | tf_op jit(solution)/shard_map/combine/pallas_call | solution.py:233
  (7 shorter events, 0.1 us)
Async XLA Ops:
  7.8 69.9 %all-to-all-start = ((bf16[128,24,768]{2,1,0:T(8,128)(2,1)}), bf16[128,24,768]{2,1,0:T(8,128)(2,1)}, u32[]{:S(2)}, u32[]{:S(2)}) async-start(bf16[128,24,768]{2,1,0:T(8,128)(2,1)} %bitcast.41), calls=%async_computation | async-start | bytes 9437184 | tf_op jit(solution)/shard_map/all_to_all | solution.py:328
  77.7 66.5 %all-to-all-start.1 = ((bf16[128,24,768]{2,1,0:T(8,128)(2,1)}), bf16[128,24,768]{2,1,0:T(8,128)(2,1)}, u32[]{:S(2)}, u32[]{:S(2)}) async-start(bf16[128,24,768]{2,1,0:T(8,128)(2,1)} %bitcast.40), calls=%async_computation.1 | async-start | bytes 9437184 | tf_op jit(solution)/shard_map/all_to_all | solution.py:328
  168.8 9.2 %copy-start.1 = (bf16[768,720]{1,0:T(8,128)(2,1)S(1)}, bf16[768,720]{1,0:T(8,128)(2,1)}, u32[]{:S(2)}) copy-start(bf16[768,720]{1,0:T(8,128)(2,1)} %get-tuple-element.19.hidden_hbm) | copy-start | bytes 3317764
  168.8 66.7 %all-to-all-start.2 = ((bf16[128,24,768]{2,1,0:T(8,128)(2,1)}), bf16[128,24,768]{2,1,0:T(8,128)(2,1)}, u32[]{:S(2)}, u32[]{:S(2)}) async-start(bf16[128,24,768]{2,1,0:T(8,128)(2,1)} %bitcast.46), calls=%async_computation.2 | async-start | bytes 9437184 | tf_op jit(solution)/shard_map/all_to_all | solution.py:328
  177.6 8.3 %slice-start = ((s8[4521984]{0:T(1024)(128)(4,1)}), s8[4194304]{0:T(1024)(128)(4,1)S(1)}, s32[]{:S(2)}) async-start(s8[4521984]{0:T(1024)(128)(4,1)} %bitcast.50), calls=%async_computation.3 | async-start | bytes 8388608
  177.9 7.9 %slice-start.1 = ((s8[4521984]{0:T(1024)(128)(4,1)}), s8[327680]{0:T(1024)(128)(4,1)S(1)}, s32[]{:S(2)}) async-start(s8[4521984]{0:T(1024)(128)(4,1)} %bitcast.50), calls=%async_computation.4 | async-start | bytes 655360
  177.9 7.9 %copy-start.3 = (bf16[768,720]{1,0:T(8,128)(2,1)S(1)}, bf16[768,720]{1,0:T(8,128)(2,1)}, u32[]{:S(2)}) copy-start(bf16[768,720]{1,0:T(8,128)(2,1)} %get-tuple-element.27) | copy-start | bytes 3317764
  185.8 5.2 %copy-start.2 = (bf16[768,720]{1,0:T(8,128)(2,1)S(1)}, bf16[768,720]{1,0:T(8,128)(2,1)}, u32[]{:S(2)}) copy-start(bf16[768,720]{1,0:T(8,128)(2,1)} %get-tuple-element.26) | copy-start | bytes 3317764
  191.1 44.4 %copy-start = (f32[128,4]{0,1:T(4,128)S(1)}, f32[128,4]{0,1:T(4,128)}, u32[]{:S(2)}) copy-start(f32[128,4]{0,1:T(4,128)} %param.12) | copy-start | bytes 6148

commit v2 on v1

v2 whole, which is shorter than its diff:
```python
import functools

import jax
import jax.numpy as jnp
from jax import lax
from jax.experimental import pallas as pl
from jax.experimental.pallas import tpu as pltpu
from jax.sharding import PartitionSpec as P

ALPHA = 1.702
CHUNKS = 4
GROUP = 8
HALVES = 2
PIECES = 4
BF = jnp.bfloat16
F32 = jnp.float32
NT = (((1,), (1,)), ((), ()))
NN = (((1,), (0,)), ((), ()))
TN = (((0,), (0,)), ((), ()))
ANY = pl.BlockSpec(memory_space=pl.ANY)
VMEM = pl.BlockSpec(memory_space=pltpu.VMEM)
PARAMS = pltpu.CompilerParams(vmem_limit_bytes=60 * 1024 * 1024)


def sort_rows(recv, pick, out, p, pieces, part, width):
    size = pick.shape[0]
    lane_rows = size // CHUNKS
    groups = recv.shape[0] // GROUP

    def step(b, carry):
        blk = recv[pl.ds(b * GROUP, GROUP)].reshape(size, part)
        picked = lax.dot_general(pick, blk, NN, preferred_element_type=F32).astype(BF)
        at = pl.ds(pl.multiple_of(b * lane_rows, lane_rows), lane_rows)
        for c in range(CHUNKS):
            w = min(part, width - c * part)
            out[at, c * part : c * part + w] = picked[c * lane_rows : (c + 1) * lane_rows, :w]
        return carry

    lax.fori_loop(p * groups // pieces, (p + 1) * groups // pieces, step, 0, unroll=2)


def expert_kernel(
    part, recv_hbm, order, order_t, wg_hbm, wu_hbm, wd_hbm,
    ret_hbm, rows_hbm, weighted_hbm, hidden_hbm, gate_hbm, up_hbm,
    recv_t, recv_c, wg, wu, wd, rows, weighted, hidden, glu, slope, gate_grad, up_grad, wide, ret,
    in_sems, t_sems, c_sems, out_sems,
):
    units, width = wg.shape
    total = rows.shape[0]
    m = total // HALVES
    last = width - (CHUNKS - 1) * part
    mark = -(-last // 128) * 128
    size = order.shape[0]
    lane_rows = size // CHUNKS
    block = recv_t.shape[1]
    sources = recv_t.shape[0]
    span = sources // PIECES

    def pieces(dst, first, sems):
        return [
            pltpu.make_async_copy(
                recv_hbm.at[pl.ds(p * span, span), pl.ds(first, block)], dst.at[pl.ds(p * span, span)], sems.at[p]
            )
            for p in range(PIECES)
        ]

    def load(src, dst, i):
        return pltpu.make_async_copy(src, dst, in_sems.at[i])

    stores = []

    def store(src, dst):
        stores.append(pltpu.make_async_copy(src, dst, out_sems.at[len(stores)]))
        stores[-1].start()

    t_loads = pieces(recv_t, 0, t_sems)
    c_loads = pieces(recv_c, block, c_sems)
    g_load, u_load, d_load = load(wg_hbm, wg, 0), load(wu_hbm, wu, 1), load(wd_hbm, wd, 2)
    for copy in (*t_loads, g_load, u_load, *c_loads, d_load):
        copy.start()
    pick = order[...]
    pick_t = order_t[...]
    for p in range(PIECES):
        t_loads[p].wait()
        sort_rows(recv_t, pick, rows, p, PIECES, part, width)
    store(rows, rows_hbm)
    for i in range(HALVES):
        at = pl.ds(i * m, m)
        if i == 0:
            g_load.wait()
        g = lax.dot_general(rows[at, :], wg[...], NT, preferred_element_type=F32)
        if i == 0:
            u_load.wait()
        u = lax.dot_general(rows[at, :], wu[...], NT, preferred_element_type=F32) + 1.0
        s = jax.nn.sigmoid(ALPHA * g)
        gl = g * s
        hidden[at, :] = (u * gl).astype(BF)
        glu[at, :] = gl
        slope[at, :] = u * (s + ALPHA * g * s * (1.0 - s))
    store(hidden, hidden_hbm)
    for p in range(PIECES):
        c_loads[p].wait()
        sort_rows(recv_c, pick, weighted, p, PIECES, part, width)
    store(weighted, weighted_hbm)
    for i in range(HALVES):
        at = pl.ds(i * m, m)
        if i == 0:
            d_load.wait()
        hg = lax.dot_general(weighted[at, :], wd[...], NT, preferred_element_type=F32)
        sg = jnp.sum(hg * hidden[at, :].astype(F32), axis=1, keepdims=True)
        ug = (hg * glu[at, :]).astype(BF)
        gg = (hg * slope[at, :]).astype(BF)
        gate_grad[at, :] = gg
        up_grad[at, :] = ug
        store(gate_grad.at[at], gate_hbm.at[at])
        store(up_grad.at[at], up_hbm.at[at])
        low = sg - sg.astype(BF).astype(F32)
        lane = lax.broadcasted_iota(jnp.int32, (m, part - mark), 1)
        tail = jnp.where(lane == 0, sg, jnp.where(lane == 1, low, 0.0)).astype(BF)
        if last < mark:
            wide[CHUNKS - 1, :, mark - 128 : mark] = jnp.zeros((m, 128), BF)
        wide[CHUNKS - 1, :, mark:] = tail
        for c in range(CHUNKS):
            w = min(part, width - c * part)
            x = lax.dot_general(gg, wg[:, c * part : c * part + w], NN, preferred_element_type=F32)
            x = x + lax.dot_general(ug, wu[:, c * part : c * part + w], NN, preferred_element_type=F32)
            wide[c, :, :w] = x.astype(BF)
        first = i * (ret.shape[0] // HALVES)

        def put(b, carry):
            src = pl.ds(pl.multiple_of(b * lane_rows, lane_rows), lane_rows)
            blk = jnp.concatenate([wide[c, src, :] for c in range(CHUNKS)], axis=0)
            out = lax.dot_general(pick_t, blk, NN, preferred_element_type=F32)
            ret[pl.ds(pl.multiple_of(first + b * size, size), size), :] = out.astype(BF)
            return carry

        lax.fori_loop(0, m // lane_rows, put, 0, unroll=2)
        half = pl.ds(first, ret.shape[0] // HALVES)
        store(ret.at[half], ret_hbm.at[half])
    for copy in stores:
        copy.wait()


def expert(recv, order, order_t, wg, wu, wd):
    units, width = wg.shape
    sources, both, part = recv.shape
    block = both // 2
    total = sources * block // CHUNKS
    like = jax.ShapeDtypeStruct
    scratch = lambda shape, dtype=BF: pltpu.VMEM(shape, dtype)
    return pl.pallas_call(
        functools.partial(expert_kernel, part),
        out_shape=(
            like((sources * block, part), BF),
            like((total, width), BF),
            like((total, width), BF),
            like((total, units), BF),
            like((total, units), BF),
            like((total, units), BF),
        ),
        in_specs=[ANY, VMEM, VMEM, ANY, ANY, ANY],
        out_specs=(ANY,) * 6,
        scratch_shapes=[
            scratch((sources, block, part)),
            scratch((sources, block, part)),
            scratch((units, width)),
            scratch((units, width)),
            scratch((units, width)),
            scratch((total, width)),
            scratch((total, width)),
            scratch((total, units)),
            scratch((total, units), F32),
            scratch((total, units), F32),
            scratch((total, units)),
            scratch((total, units)),
            scratch((CHUNKS, total // HALVES, part)),
            scratch((sources * block, part)),
            pltpu.SemaphoreType.DMA((3,)),
            pltpu.SemaphoreType.DMA((PIECES,)),
            pltpu.SemaphoreType.DMA((PIECES,)),
            pltpu.SemaphoreType.DMA((3 + 3 * HALVES,)),
        ],
        compiler_params=PARAMS,
        name="expert",
    )(recv, order, order_t, wg, wu, wd)


def combine_kernel(part, width, back, hits, masks, probs, input_grad, prob_grad, acc, pacc):
    step = pl.program_id(0)
    tops, tok = probs.shape
    last = width - (CHUNKS - 1) * part
    mark = -(-last // 128) * 128

    @pl.when(step == 0)
    def _():
        acc[...] = jnp.zeros_like(acc)
        pacc[...] = jnp.zeros_like(pacc)

    hit = hits[...]
    own = hit[:tok]
    for k in range(1, tops):
        own = own + hit[k * tok : (k + 1) * tok]
    mask = masks[...]
    spread = jnp.concatenate([own * mask[c : c + 1] for c in range(CHUNKS)], axis=0)
    blk = back[...]
    acc[...] += lax.dot_general(spread, blk, NN, preferred_element_type=F32)
    pacc[...] += lax.dot_general(hit * mask[CHUNKS - 1 : CHUNKS], blk[:, mark : mark + 128], NN, preferred_element_type=F32)

    @pl.when(step == pl.num_programs(0) - 1)
    def _():
        for c in range(CHUNKS):
            w = min(part, width - c * part)
            input_grad[c * part : c * part + w, :] = acc[c * tok : (c + 1) * tok, :].T[:w].astype(BF)
        for k in range(tops):
            col = pacc[k * tok : (k + 1) * tok, :].T
            prob_grad[k : k + 1, :] = (col[0:1] + col[1:2]) / probs[k : k + 1, :]

def combine(back, hits, masks, probs_t, width):
    rows, part = back.shape
    tops, tok = probs_t.shape
    span = masks.shape[1]
    turns = hits.shape[1] // span
    like = jax.ShapeDtypeStruct
    return pl.pallas_call(
        functools.partial(combine_kernel, part, width),
        grid=(rows // span,),
        out_shape=(like((width, tok), BF), like((tops, tok), F32)),
        in_specs=[
            pl.BlockSpec((span, part), lambda i: (i, 0)),
            pl.BlockSpec((tops * tok, span), lambda i: (0, i % turns)),
            pl.BlockSpec((CHUNKS, span), lambda i: (0, 0)),
            pl.BlockSpec((tops, tok), lambda i: (0, 0)),
        ],
        out_specs=(pl.BlockSpec((width, tok), lambda i: (0, 0)), pl.BlockSpec((tops, tok), lambda i: (0, 0))),
        scratch_shapes=[pltpu.VMEM((CHUNKS * tok, part), F32), pltpu.VMEM((tops * tok, 128), F32)],
        compiler_params=pltpu.CompilerParams(vmem_limit_bytes=24 * 1024 * 1024),
        name="combine",
    )(back, hits, masks, probs_t)

def divide(x, by):
    return jnp.floor((x.astype(F32) + 0.5) * (1.0 / by)).astype(jnp.int32)


def build_kernel(part, capacity, tokens_t, cotangent_t, position, probs, out, wide):
    width, tok = tokens_t.shape
    tops = position.shape[0]

    @pl.when(pl.program_id(0) == 0)
    def _():
        for j, src in enumerate((tokens_t, cotangent_t)):
            for c in range(CHUNKS):
                w = min(part, width - c * part)
                wide[j, c * tok : (c + 1) * tok, :w] = src[c * part : c * part + w, :].T
                if w < part:
                    wide[j, c * tok : (c + 1) * tok, w:] = jnp.zeros((tok, part - w), BF)

    experts, both = out.shape[1:3]
    block = both // 2
    n = experts * block
    row = pl.program_id(0) * n + lax.broadcasted_iota(jnp.int32, (n, 1), 0)
    expert = divide(row, block)
    row = row - expert * block
    chunk = divide(row, capacity)
    slot = expert * capacity + row - chunk * capacity
    own = jnp.zeros((n, tok), F32)
    prob = jnp.zeros((n, tok), F32)
    for k in range(tops):
        hit = slot == position[k : k + 1, :]
        own = jnp.where(hit, 1.0, own)
        prob = jnp.where(hit, probs[k : k + 1, :], prob)
    pick = jnp.concatenate([jnp.where(chunk == c, own, 0.0).astype(BF) for c in range(CHUNKS)], axis=1)
    sent = lax.dot_general(pick, wide[0], NN, preferred_element_type=F32).astype(BF)
    cot = lax.dot_general(pick, wide[1], NN, preferred_element_type=F32)
    cot = (cot * jnp.sum(prob, axis=1, keepdims=True)).astype(BF)
    for d in range(out.shape[0]):
        out[d, :, :block, :] = sent.reshape(experts, block, part)
        out[d, :, block:, :] = cot.reshape(experts, block, part)


def build(tokens_t, cotangent_t, position, probs, capacity, experts, part, holders):
    width, tok = tokens_t.shape
    tops = position.shape[0]
    both = 2 * CHUNKS * capacity
    steps = 4
    whole = lambda shape: pl.BlockSpec(shape, lambda i: (0,) * len(shape))
    return pl.pallas_call(
        functools.partial(build_kernel, part, capacity),
        grid=(steps,),
        out_shape=jax.ShapeDtypeStruct((holders, experts, both, part), BF),
        in_specs=[whole((width, tok)), whole((width, tok)), whole((tops, tok)), whole((tops, tok))],
        out_specs=pl.BlockSpec((holders, experts // steps, both, part), lambda i: (0, i, 0, 0)),
        scratch_shapes=[pltpu.VMEM((2, CHUNKS * tok, part), BF)],
        compiler_params=PARAMS,
        name="build",
    )(tokens_t, cotangent_t, position, probs)


def body(tokens, cotangent, expert_ids, slots, probs, w_gate, w_up, w_down):
    experts = lax.axis_size("expert")
    holders = lax.axis_size("dp")
    tok_rows, width = tokens.shape
    top_count = expert_ids.shape[1]
    capacity = max(2, 3 * tok_rows * top_count // (4 * experts))
    part = -(-width // (CHUNKS * 128)) * 128
    devices = holders * experts
    block = CHUNKS * capacity
    send_rows = experts * block
    position = jnp.where(slots >= 0, expert_ids * capacity + slots, -1).T
    probs_t = probs.T

    row = jnp.arange(send_rows, dtype=jnp.int32)
    row_slot = (row // block) * capacity + row % capacity
    row_chunk = (row // capacity) % CHUNKS

    i = jnp.arange(GROUP * block, dtype=jnp.int32)
    source, chunk, slot = (i // capacity) % GROUP, i // (GROUP * capacity), i % capacity
    target = source * block + chunk * capacity + slot
    order = (target[:, None] == i[None, :]).astype(BF)
    order_t = (i[:, None] == target[None, :]).astype(BF)

    def exchange(blocks):
        return lax.all_to_all(blocks, ("dp", "expert"), split_axis=0, concat_axis=0, tiled=True)

    gate_w = w_gate[0].T
    up_w = w_up[0].T
    down_w = w_down[0].T
    sent = build(tokens.T, cotangent.T, position, probs_t, capacity, experts, part, holders)
    recv = exchange(sent.reshape(devices, 2 * block, part))
    hits = (position.reshape(top_count * tok_rows, 1) == row_slot[None, :]).astype(BF)
    masks = (row_chunk[None, : send_rows // 4] == jnp.arange(CHUNKS)[:, None]).astype(BF)
    ret, rows, weighted, hidden, gate_grad, up_grad = expert(recv, order, order_t, gate_w, up_w, down_w)
    back = exchange(ret.reshape(devices, block, part)).reshape(devices * block, part)
    with jax.named_scope("weight_grads"):
        grad_down = lax.dot_general(weighted, hidden, TN, preferred_element_type=F32).astype(BF)
        grad_gate = lax.dot_general(rows, gate_grad, TN, preferred_element_type=F32).astype(BF)
        grad_up = lax.dot_general(rows, up_grad, TN, preferred_element_type=F32).astype(BF)
    with jax.named_scope("combine"):
        input_grad, prob_grad = combine(back, hits, masks, probs_t, width)
    return (input_grad.T, prob_grad.T, grad_gate[None], grad_up[None], grad_down[None])


def solution(mesh):
    tokens = P(("expert", "dp"), None)
    weights = P("expert", None, "dp")
    return jax.shard_map(
        body,
        mesh=mesh,
        in_specs=(tokens,) * 5 + (weights,) * 3,
        out_specs=(tokens,) * 2 + (weights,) * 3,
        check_vma=False,
    )
```

time: 246 us -> 258 us (1.049)
  waiting for transfers between devices: 130 us -> 155 us
  Pallas kernels: 63.6 us -> 51.1 us
    all_to_all x3 -> x2, waiting for transfers between devices: 130 us -> 155 us  [exchange(): lax.all_to_all(blocks, ('dp', 'expert'), split_axis=0, concat_axis=0, til...]
    pallas_call x4 -> x2, Pallas kernels: 54.5 us -> 42 us  [the longest x1 34.7 us: expert(): pl.pallas_call(functools.partial(expert_kernel, part), out_shape=(like((s...]
    dot_general x1, matrix products: 5.23 us -> 7.89 us  [body(): lax.dot_general(rows, up_grad, TN, preferred_element_type=F32).astype(BF)]
    dot_general x1, matrix products: 7.88 us -> 5.23 us  [body(): lax.dot_general(weighted, hidden, TN, preferred_element_type=F32).astype(BF)]
    all_to_all x3 -> x2, starting transfers between devices: 29.2 us -> 28.4 us  [exchange(): lax.all_to_all(blocks, ('dp', 'expert'), split_axis=0, concat_axis=0, til...]
  transfers between devices with their start and end apart: 3 -> 2, of which waited for: 3 -> 2; matrix products, arithmetic and copies ran while one was open for 8% -> 8% of each run, Pallas kernels for 10% -> 0%
where the time goes in v2:
time: 258 us; the launch traced here: 256 us
  waiting for transfers between devices  155 us (60%)
  Pallas kernels  51.1 us (20%)
  starting transfers between devices  28.4 us (11%)
  matrix products  18.3 us (7%)
    all_to_all x2, waiting for transfers between devices, exchange(): lax.all_to_all(blocks, ('dp', 'expert'), split_axis=0, concat_axis=0, til...  155 us
    pallas_call x1, Pallas kernels, expert(): pl.pallas_call(functools.partial(expert_kernel, part), out_shape=(like((s...  34.7 us
    all_to_all x2, starting transfers between devices, exchange(): lax.all_to_all(blocks, ('dp', 'expert'), split_axis=0, concat_axis=0, til...  28.4 us
    pallas_call x1, Pallas kernels, combine(): pl.pallas_call(functools.partial(combine_kernel, part, width), grid=(rows...  9.13 us
    dot_general x1, matrix products, body(): lax.dot_general(rows, up_grad, TN, preferred_element_type=F32).astype(BF)  7.89 us
    pallas_call x1, Pallas kernels, build(): pl.pallas_call(functools.partial(build_kernel, part, capacity), grid=(ste...  7.27 us
    dot_general x1, matrix products, body(): lax.dot_general(weighted, hidden, TN, preferred_element_type=F32).astype(BF)  5.23 us
    dot_general x1, matrix products, body(): lax.dot_general(rows, gate_grad, TN, preferred_element_type=F32).astype(BF)  5.23 us
  transfers between devices with their start and end apart: 2, of which 2 were waited for; matrix products, arithmetic and copies ran while one was open for 8% of the time, Pallas kernels for 0%

profile of v2, /device:TPU:1, one launch (start us, length us, event | category | flops | bytes accessed | tf_op | source)
XLA Modules:
  0.0 256.3 jit_solution(17237869458719231657)
XLA Ops:
  0.6 1.3 fusion.25
  1.9 7.3 %build.1 = bf16[2,64,48,768]{3,2,1,0:T(8,128)(2,1)} custom-call(bf16[2880,128]{1,0:T(8,128)(2,1)} %bitcast.41, bf16[2880,128]{1,0:T(8,128)(2,1)} %bitcast.42, s32[4,128]{1,0:T(4,128)} %get-tuple-element.22.position, f32[4,128]{1,0:T(4,128)} %bitcast.34), custom_call_target="tpu_custom_call" | custom-call | tf_op jit(solution)/shard_map/build/pallas_call | solution.py:286
  9.2 11.9 %all-to-all-start = ((bf16[128,48,768]{2,1,0:T(8,128)(2,1)}), bf16[128,48,768]{2,1,0:T(8,128)(2,1)}, u32[]{:S(2)}, u32[]{:S(2)}) async-start(bf16[128,48,768]{2,1,0:T(8,128)(2,1)} %bitcast.36), calls=%async_computation | async-start | bytes 18874368 | tf_op jit(solution)/shard_map/all_to_all | solution.py:322
  21.1 0.7 fusion.4
  21.8 116.1 %all-to-all-done.recv_hbm = bf16[128,48,768]{2,1,0:T(8,128)(2,1)} async-done(((bf16[128,48,768]{2,1,0:T(8,128)(2,1)}), bf16[128,48,768]{2,1,0:T(8,128)(2,1)}, u32[]{:S(2)}, u32[]{:S(2)}) %all-to-all-start) | async-done | bytes 9437216 | tf_op jit(solution)/shard_map/all_to_all | solution.py:322
  137.9 34.7 %expert.1 = (bf16[3072,768]{1,0:T(8,128)(2,1)}, bf16[768,2880]{1,0:T(8,128)(2,1)}, bf16[768,2880]{1,0:T(8,128)(2,1)}, bf16[768,720]{1,0:T(8,128)(2,1)}, bf16[768...) custom-call(bf16[128,48,768]{2,1,0:T(8,128)(2,1)} %all-to-all-done.recv_hbm, bf16[192,192]{1,0:T(8,128)(2,1)} %get-tuple-element.24.order, ...), custom_call_target="tpu_custom_call" | custom-call | tf_op jit(solution)/shard_map/expert/pallas_call | solution.py:151
  172.7 0.0 copy-start.3
  172.7 16.5 %all-to-all-start.1 = ((bf16[128,24,768]{2,1,0:T(8,128)(2,1)}), bf16[128,24,768]{2,1,0:T(8,128)(2,1)}, u32[]{:S(2)}, u32[]{:S(2)}) async-start(bf16[128,24,768]{2,1,0:T(8,128)(2,1)} %bitcast.37), calls=%async_computation.1 | async-start | bytes 9437184 | tf_op jit(solution)/shard_map/all_to_all | solution.py:322
  189.3 0.0 slice-start.2
  189.3 0.3 compare_convert_fusion.hits
  189.7 0.0 copy-done.3
  189.7 0.0 slice-start.3
  189.7 0.0 copy-start.2
  189.7 0.0 slice-start
  189.7 7.9 %fusion.1 = bf16[1,2880,720]{1,2,0:T(8,128)(2,1)} fusion(bf16[768,2880]{1,0:T(8,128)(2,1)} %get-tuple-element.16, bf16[768,720]{1,0:T(8,128)(2,1)S(1)} %copy-done.3), kind=kOutput, calls=%fused_computation.4 | convolution fusion | flops 3187123200 | bytes 9676800 | tf_op jit(solution)/shard_map/weight_grads/dot_general | solution.py:336
  197.6 0.0 slice-done.2
  197.6 0.0 slice-done.3
  197.6 0.0 copy-done.2
  197.6 0.0 slice-start.1
  197.6 0.0 copy-start.1
  197.6 5.2 %fusion = bf16[1,2880,720]{1,2,0:T(8,128)(2,1)} fusion(bf16[768,2880]{1,0:T(8,128)(2,1)S(1)} %bitcast.46, bf16[768,720]{1,0:T(8,128)(2,1)S(1)} %copy-done.2), kind=kOutput, calls=%fused_computation.3 | convolution fusion | flops 3187123200 | bytes 9676800 | tf_op jit(solution)/shard_map/weight_grads/dot_general | solution.py:335
  202.9 0.0 slice-done
  202.9 0.0 slice-done.1
  202.9 0.0 copy-done.1
  202.9 0.0 copy-start
  202.9 5.2 %fusion.2 = bf16[1,2880,720]{1,2,0:T(8,128)(2,1)} fusion(bf16[768,2880]{1,0:T(8,128)(2,1)S(1)} %bitcast.44, bf16[768,720]{1,0:T(8,128)(2,1)S(1)} %copy-done.1), kind=kOutput, calls=%fused_computation.5 | convolution fusion | flops 3187123200 | bytes 9676800 | tf_op jit(solution)/shard_map/weight_grads/dot_general | solution.py:334
  208.1 39.1 %all-to-all-done.1 = bf16[128,24,768]{2,1,0:T(8,128)(2,1)} async-done(((bf16[128,24,768]{2,1,0:T(8,128)(2,1)}), bf16[128,24,768]{2,1,0:T(8,128)(2,1)}, u32[]{:S(2)}, u32[]{:S(2)}) %all-to-all-start.1) | async-done | bytes 4718624 | tf_op jit(solution)/shard_map/all_to_all | solution.py:322
  247.2 0.0 copy-done
  247.2 9.1 %combine.1 = (bf16[2880,128]{1,0:T(8,128)(2,1)}, f32[4,128]{1,0:T(4,128)}) custom-call(bf16[3072,768]{1,0:T(8,128)(2,1)} %bitcast.12.back, bf16[512,1536]{1,0:T(8,128)(2,1)S(1)} %compare_convert_fusion.hits, bf16[4,384]{1,0:T(4,128)(2,1)S(1)} %fusion.16.masks, f32[4,128]{1,0:T(4,128)S(1)} %bitcast.35), custom_call_target="tpu_custom_call" | custom-call | tf_op jit(solution)/shard_map/combine/combine/pallas_call | solution.py:224
  (8 shorter events, 0.1 us)
Async XLA Ops:
  9.2 128.8 %all-to-all-start = ((bf16[128,48,768]{2,1,0:T(8,128)(2,1)}), bf16[128,48,768]{2,1,0:T(8,128)(2,1)}, u32[]{:S(2)}, u32[]{:S(2)}) async-start(bf16[128,48,768]{2,1,0:T(8,128)(2,1)} %bitcast.36), calls=%async_computation | async-start | bytes 18874368 | tf_op jit(solution)/shard_map/all_to_all | solution.py:322
  172.7 17.0 %copy-start.3 = (bf16[768,720]{1,0:T(8,128)(2,1)S(1)}, bf16[768,720]{1,0:T(8,128)(2,1)}, u32[]{:S(2)}) copy-start(bf16[768,720]{1,0:T(8,128)(2,1)} %get-tuple-element.18) | copy-start | bytes 3317764
  172.7 74.5 %all-to-all-start.1 = ((bf16[128,24,768]{2,1,0:T(8,128)(2,1)}), bf16[128,24,768]{2,1,0:T(8,128)(2,1)}, u32[]{:S(2)}, u32[]{:S(2)}) async-start(bf16[128,24,768]{2,1,0:T(8,128)(2,1)} %bitcast.37), calls=%async_computation.1 | async-start | bytes 9437184 | tf_op jit(solution)/shard_map/all_to_all | solution.py:322
  189.3 8.3 %slice-start.2 = ((s8[4521984]{0:T(1024)(128)(4,1)}), s8[4194304]{0:T(1024)(128)(4,1)S(1)}, s32[]{:S(2)}) async-start(s8[4521984]{0:T(1024)(128)(4,1)} %bitcast.45), calls=%async_computation.4 | async-start | bytes 8388608
  189.7 7.9 %slice-start.3 = ((s8[4521984]{0:T(1024)(128)(4,1)}), s8[327680]{0:T(1024)(128)(4,1)S(1)}, s32[]{:S(2)}) async-start(s8[4521984]{0:T(1024)(128)(4,1)} %bitcast.45), calls=%async_computation.5 | async-start | bytes 655360
  189.7 7.9 %copy-start.2 = (bf16[768,720]{1,0:T(8,128)(2,1)S(1)}, bf16[768,720]{1,0:T(8,128)(2,1)}, u32[]{:S(2)}) copy-start(bf16[768,720]{1,0:T(8,128)(2,1)} %get-tuple-element.17) | copy-start | bytes 3317764
  189.7 13.2 %slice-start = ((s8[4521984]{0:T(1024)(128)(4,1)}), s8[4194304]{0:T(1024)(128)(4,1)S(1)}, s32[]{:S(2)}) async-start(s8[4521984]{0:T(1024)(128)(4,1)} %bitcast.43), calls=%async_computation.2 | async-start | bytes 8388608
  197.6 5.3 %slice-start.1 = ((s8[4521984]{0:T(1024)(128)(4,1)}), s8[327680]{0:T(1024)(128)(4,1)S(1)}, s32[]{:S(2)}) async-start(s8[4521984]{0:T(1024)(128)(4,1)} %bitcast.43), calls=%async_computation.3 | async-start | bytes 655360
  197.6 5.3 %copy-start.1 = (bf16[768,720]{1,0:T(8,128)(2,1)S(1)}, bf16[768,720]{1,0:T(8,128)(2,1)}, u32[]{:S(2)}) copy-start(bf16[768,720]{1,0:T(8,128)(2,1)} %get-tuple-element.20) | copy-start | bytes 3317764
  202.9 44.3 %copy-start = (f32[128,4]{0,1:T(4,128)S(1)}, f32[128,4]{0,1:T(4,128)}, u32[]{:S(2)}) copy-start(f32[128,4]{0,1:T(4,128)} %param.12) | copy-start | bytes 6148

commit v3 on v2

--- a/solution.py
+++ b/solution.py
@@ -2,6 +2,7 @@
 
 import jax
 import jax.numpy as jnp
+import numpy as np
 from jax import lax
 from jax.experimental import pallas as pl
 from jax.experimental.pallas import tpu as pltpu
@@ -312,11 +313,11 @@
     row_slot = (row // block) * capacity + row % capacity
     row_chunk = (row // capacity) % CHUNKS
 
-    i = jnp.arange(GROUP * block, dtype=jnp.int32)
+    i = np.arange(GROUP * block)
     source, chunk, slot = (i // capacity) % GROUP, i // (GROUP * capacity), i % capacity
     target = source * block + chunk * capacity + slot
-    order = (target[:, None] == i[None, :]).astype(BF)
-    order_t = (i[:, None] == target[None, :]).astype(BF)
+    order = jnp.asarray(target[:, None] == i[None, :], BF)
+    order_t = jnp.asarray(i[:, None] == target[None, :], BF)
 
     def exchange(blocks):
         return lax.all_to_all(blocks, ("dp", "expert"), split_axis=0, concat_axis=0, tiled=True)

time: 258 us -> 245 us (0.950)
  blocking collectives: 0 us -> 122 us
  waiting for transfers between devices: 155 us -> 39.1 us
  starting transfers between devices: 28.4 us -> 10.5 us
    all_to_all x0 -> x1, blocking collectives: none -> 122 us  [exchange(): lax.all_to_all(blocks, ('dp', 'expert'), split_axis=0, concat_axis=0, til...]
    all_to_all x2 -> x1, waiting for transfers between devices: 155 us -> 39.1 us  [exchange(): lax.all_to_all(blocks, ('dp', 'expert'), split_axis=0, concat_axis=0, til...]
    all_to_all x2 -> x1, starting transfers between devices: 28.4 us -> 10.5 us  [exchange(): lax.all_to_all(blocks, ('dp', 'expert'), split_axis=0, concat_axis=0, til...]
  transfers between devices with their start and end apart: 2 -> 1, of which waited for: 2 -> 1; matrix products, arithmetic and copies ran while one was open for 8% -> 8% of each run, Pallas kernels for 0% -> 0%
where the time goes in v3:
time: 245 us; the launch traced here: 243 us
  blocking collectives  122 us (50%)
  Pallas kernels  51.2 us (21%)
  waiting for transfers between devices  39.1 us (16%)
  matrix products  18.3 us (7%)
  starting transfers between devices  10.5 us (4%)
    all_to_all x1, blocking collectives, exchange(): lax.all_to_all(blocks, ('dp', 'expert'), split_axis=0, concat_axis=0, til...  122 us
    all_to_all x1, waiting for transfers between devices, exchange(): lax.all_to_all(blocks, ('dp', 'expert'), split_axis=0, concat_axis=0, til...  39.1 us
    pallas_call x1, Pallas kernels, expert(): pl.pallas_call(functools.partial(expert_kernel, part), out_shape=(like((s...  34.7 us
    all_to_all x1, starting transfers between devices, exchange(): lax.all_to_all(blocks, ('dp', 'expert'), split_axis=0, concat_axis=0, til...  10.5 us
    pallas_call x1, Pallas kernels, combine(): pl.pallas_call(functools.partial(combine_kernel, part, width), grid=(rows...  9.13 us
    dot_general x1, matrix products, body(): lax.dot_general(rows, up_grad, TN, preferred_element_type=F32).astype(BF)  7.88 us
    pallas_call x1, Pallas kernels, build(): pl.pallas_call(functools.partial(build_kernel, part, capacity), grid=(ste...  7.29 us
    dot_general x1, matrix products, body(): lax.dot_general(weighted, hidden, TN, preferred_element_type=F32).astype(BF)  5.21 us
  transfers between devices with their start and end apart: 1, of which 1 were waited for; matrix products, arithmetic and copies ran while one was open for 8% of the time, Pallas kernels for 0%

profile of v3, /device:TPU:1, one launch (start us, length us, event | category | flops | bytes accessed | tf_op | source)
XLA Modules:
  0.0 243.2 jit_solution(10998445058475816319)
XLA Ops:
  0.6 1.3 fusion.15
  1.9 7.3 %build.1 = bf16[2,64,48,768]{3,2,1,0:T(8,128)(2,1)} custom-call(bf16[2880,128]{1,0:T(8,128)(2,1)} %bitcast.41, bf16[2880,128]{1,0:T(8,128)(2,1)} %bitcast.42, s32[4,128]{1,0:T(4,128)} %get-tuple-element.22.position, f32[4,128]{1,0:T(4,128)} %bitcast.34), custom_call_target="tpu_custom_call" | custom-call | tf_op jit(solution)/shard_map/build/pallas_call | solution.py:287
  9.2 121.7 %all_to_all.10.recv_hbm = bf16[128,48,768]{2,1,0:T(8,128)(2,1)} all-to-all(bf16[128,48,768]{2,1,0:T(8,128)(2,1)} %bitcast.36), channel_id=1, replica_groups=mesh['expert'=64,'dp'=2] {'dp','expert'}, dimensions={0} | all-to-all | bytes 18874368 | tf_op jit(solution)/shard_map/all_to_all | solution.py:323
  130.9 34.7 %expert.1 = (bf16[3072,768]{1,0:T(8,128)(2,1)}, bf16[768,2880]{1,0:T(8,128)(2,1)}, bf16[768,2880]{1,0:T(8,128)(2,1)}, bf16[768,720]{1,0:T(8,128)(2,1)}, bf16[768...) custom-call(bf16[128,48,768]{2,1,0:T(8,128)(2,1)} %all_to_all.10.recv_hbm, bf16[192,192]{1,0:T(8,128)(2,1)} %constant.45.clone.order, ...), custom_call_target="tpu_custom_call" | custom-call | tf_op jit(solution)/shard_map/expert/pallas_call | solution.py:152
  165.6 0.0 copy-start.3
  165.6 10.5 %all-to-all-start.1 = ((bf16[128,24,768]{2,1,0:T(8,128)(2,1)}), bf16[128,24,768]{2,1,0:T(8,128)(2,1)}, u32[]{:S(2)}, u32[]{:S(2)}) async-start(bf16[128,24,768]{2,1,0:T(8,128)(2,1)} %bitcast.37), calls=%async_computation.1 | async-start | bytes 9437184 | tf_op jit(solution)/shard_map/all_to_all | solution.py:323
  176.2 0.0 slice-start.2
  176.2 0.3 compare_convert_fusion.hits
  176.6 0.0 copy-done.3
  176.6 0.0 slice-start.3
  176.6 0.0 copy-start.2
  176.6 0.0 slice-start
  176.6 7.9 %fusion.1 = bf16[1,2880,720]{1,2,0:T(8,128)(2,1)} fusion(bf16[768,2880]{1,0:T(8,128)(2,1)} %get-tuple-element.16, bf16[768,720]{1,0:T(8,128)(2,1)S(1)} %copy-done.3), kind=kOutput, calls=%fused_computation.4 | convolution fusion | flops 3187123200 | bytes 9676800 | tf_op jit(solution)/shard_map/weight_grads/dot_general | solution.py:337
  184.5 0.0 slice-done.2
  184.5 0.0 slice-done.3
  184.5 0.0 copy-done.2
  184.5 0.0 slice-start.1
  184.5 0.0 copy-start.1
  184.5 5.2 %fusion = bf16[1,2880,720]{1,2,0:T(8,128)(2,1)} fusion(bf16[768,2880]{1,0:T(8,128)(2,1)S(1)} %bitcast.46, bf16[768,720]{1,0:T(8,128)(2,1)S(1)} %copy-done.2), kind=kOutput, calls=%fused_computation.3 | convolution fusion | flops 3187123200 | bytes 9676800 | tf_op jit(solution)/shard_map/weight_grads/dot_general | solution.py:336
  189.7 0.0 slice-done
  189.7 0.0 slice-done.1
  189.7 0.0 copy-done.1
  189.8 0.0 copy-start
  189.8 5.2 %fusion.2 = bf16[1,2880,720]{1,2,0:T(8,128)(2,1)} fusion(bf16[768,2880]{1,0:T(8,128)(2,1)S(1)} %bitcast.44, bf16[768,720]{1,0:T(8,128)(2,1)S(1)} %copy-done.1), kind=kOutput, calls=%fused_computation.5 | convolution fusion | flops 3187123200 | bytes 9676800 | tf_op jit(solution)/shard_map/weight_grads/dot_general | solution.py:335
  195.0 39.1 %all-to-all-done.1 = bf16[128,24,768]{2,1,0:T(8,128)(2,1)} async-done(((bf16[128,24,768]{2,1,0:T(8,128)(2,1)}), bf16[128,24,768]{2,1,0:T(8,128)(2,1)}, u32[]{:S(2)}, u32[]{:S(2)}) %all-to-all-start.1) | async-done | bytes 4718624 | tf_op jit(solution)/shard_map/all_to_all | solution.py:323
  234.1 0.0 copy-done
  234.1 9.1 %combine.1 = (bf16[2880,128]{1,0:T(8,128)(2,1)}, f32[4,128]{1,0:T(4,128)}) custom-call(bf16[3072,768]{1,0:T(8,128)(2,1)} %bitcast.12.back, bf16[512,1536]{1,0:T(8,128)(2,1)S(1)} %compare_convert_fusion.hits, bf16[4,384]{1,0:T(4,128)(2,1)S(1)} %fusion.14.masks, f32[4,128]{1,0:T(4,128)S(1)} %bitcast.35), custom_call_target="tpu_custom_call" | custom-call | tf_op jit(solution)/shard_map/combine/combine/pallas_call | solution.py:225
  (7 shorter events, 0.1 us)
Async XLA Ops:
  165.6 11.0 %copy-start.3 = (bf16[768,720]{1,0:T(8,128)(2,1)S(1)}, bf16[768,720]{1,0:T(8,128)(2,1)}, u32[]{:S(2)}) copy-start(bf16[768,720]{1,0:T(8,128)(2,1)} %get-tuple-element.18) | copy-start | bytes 3317764
  165.6 68.5 %all-to-all-start.1 = ((bf16[128,24,768]{2,1,0:T(8,128)(2,1)}), bf16[128,24,768]{2,1,0:T(8,128)(2,1)}, u32[]{:S(2)}, u32[]{:S(2)}) async-start(bf16[128,24,768]{2,1,0:T(8,128)(2,1)} %bitcast.37), calls=%async_computation.1 | async-start | bytes 9437184 | tf_op jit(solution)/shard_map/all_to_all | solution.py:323
  176.2 8.3 %slice-start.2 = ((s8[4521984]{0:T(1024)(128)(4,1)}), s8[4194304]{0:T(1024)(128)(4,1)S(1)}, s32[]{:S(2)}) async-start(s8[4521984]{0:T(1024)(128)(4,1)} %bitcast.45), calls=%async_computation.4 | async-start | bytes 8388608
  176.6 7.9 %slice-start.3 = ((s8[4521984]{0:T(1024)(128)(4,1)}), s8[327680]{0:T(1024)(128)(4,1)S(1)}, s32[]{:S(2)}) async-start(s8[4521984]{0:T(1024)(128)(4,1)} %bitcast.45), calls=%async_computation.5 | async-start | bytes 655360
  176.6 7.9 %copy-start.2 = (bf16[768,720]{1,0:T(8,128)(2,1)S(1)}, bf16[768,720]{1,0:T(8,128)(2,1)}, u32[]{:S(2)}) copy-start(bf16[768,720]{1,0:T(8,128)(2,1)} %get-tuple-element.17) | copy-start | bytes 3317764
  176.6 13.2 %slice-start = ((s8[4521984]{0:T(1024)(128)(4,1)}), s8[4194304]{0:T(1024)(128)(4,1)S(1)}, s32[]{:S(2)}) async-start(s8[4521984]{0:T(1024)(128)(4,1)} %bitcast.43), calls=%async_computation.2 | async-start | bytes 8388608
  184.5 5.2 %slice-start.1 = ((s8[4521984]{0:T(1024)(128)(4,1)}), s8[327680]{0:T(1024)(128)(4,1)S(1)}, s32[]{:S(2)}) async-start(s8[4521984]{0:T(1024)(128)(4,1)} %bitcast.43), calls=%async_computation.3 | async-start | bytes 655360
  184.5 5.2 %copy-start.1 = (bf16[768,720]{1,0:T(8,128)(2,1)S(1)}, bf16[768,720]{1,0:T(8,128)(2,1)}, u32[]{:S(2)}) copy-start(bf16[768,720]{1,0:T(8,128)(2,1)} %get-tuple-element.20) | copy-start | bytes 3317764
  189.8 44.3 %copy-start = (f32[128,4]{0,1:T(4,128)S(1)}, f32[128,4]{0,1:T(4,128)}, u32[]{:S(2)}) copy-start(f32[128,4]{0,1:T(4,128)} %param.14) | copy-start | bytes 6148

commit v4 on v3

--- a/solution.py
+++ b/solution.py
@@ -12,7 +12,10 @@
 CHUNKS = 4
 GROUP = 8
 HALVES = 2
-PIECES = 4
+PARTS = 2
+UNROLL = 8
+STEPS = 4
+TURNS = 1
 BF = jnp.bfloat16
 F32 = jnp.float32
 NT = (((1,), (1,)), ((), ()))
@@ -23,7 +26,7 @@
 PARAMS = pltpu.CompilerParams(vmem_limit_bytes=60 * 1024 * 1024)
 
 
-def sort_rows(recv, pick, out, p, pieces, part, width):
+def sort_rows(recv, pick, out, i, part, width):
     size = pick.shape[0]
     lane_rows = size // CHUNKS
     groups = recv.shape[0] // GROUP
@@ -37,7 +40,7 @@
             out[at, c * part : c * part + w] = picked[c * lane_rows : (c + 1) * lane_rows, :w]
         return carry
 
-    lax.fori_loop(p * groups // pieces, (p + 1) * groups // pieces, step, 0, unroll=2)
+    lax.fori_loop(i * groups // HALVES, (i + 1) * groups // HALVES, step, 0, unroll=UNROLL)
 
 
 def expert_kernel(
@@ -55,14 +58,14 @@
     lane_rows = size // CHUNKS
     block = recv_t.shape[1]
     sources = recv_t.shape[0]
-    span = sources // PIECES
+    span = sources // HALVES
 
     def pieces(dst, first, sems):
         return [
             pltpu.make_async_copy(
                 recv_hbm.at[pl.ds(p * span, span), pl.ds(first, block)], dst.at[pl.ds(p * span, span)], sems.at[p]
             )
-            for p in range(PIECES)
+            for p in range(HALVES)
         ]
 
     def load(src, dst, i):
@@ -77,16 +80,15 @@
     t_loads = pieces(recv_t, 0, t_sems)
     c_loads = pieces(recv_c, block, c_sems)
     g_load, u_load, d_load = load(wg_hbm, wg, 0), load(wu_hbm, wu, 1), load(wd_hbm, wd, 2)
-    for copy in (*t_loads, g_load, u_load, *c_loads, d_load):
+    for copy in (t_loads[0], g_load, u_load, *t_loads[1:], d_load, *c_loads):
         copy.start()
     pick = order[...]
     pick_t = order_t[...]
-    for p in range(PIECES):
-        t_loads[p].wait()
-        sort_rows(recv_t, pick, rows, p, PIECES, part, width)
-    store(rows, rows_hbm)
     for i in range(HALVES):
         at = pl.ds(i * m, m)
+        t_loads[i].wait()
+        sort_rows(recv_t, pick, rows, i, part, width)
+        store(rows.at[at], rows_hbm.at[at])
         if i == 0:
             g_load.wait()
         g = lax.dot_general(rows[at, :], wg[...], NT, preferred_element_type=F32)
@@ -98,13 +100,12 @@
         hidden[at, :] = (u * gl).astype(BF)
         glu[at, :] = gl
         slope[at, :] = u * (s + ALPHA * g * s * (1.0 - s))
-    store(hidden, hidden_hbm)
-    for p in range(PIECES):
-        c_loads[p].wait()
-        sort_rows(recv_c, pick, weighted, p, PIECES, part, width)
-    store(weighted, weighted_hbm)
+        store(hidden.at[at], hidden_hbm.at[at])
     for i in range(HALVES):
         at = pl.ds(i * m, m)
+        c_loads[i].wait()
+        sort_rows(recv_c, pick, weighted, i, part, width)
+        store(weighted.at[at], weighted_hbm.at[at])
         if i == 0:
             d_load.wait()
         hg = lax.dot_general(weighted[at, :], wd[...], NT, preferred_element_type=F32)
@@ -135,9 +136,11 @@
             ret[pl.ds(pl.multiple_of(first + b * size, size), size), :] = out.astype(BF)
             return carry
 
-        lax.fori_loop(0, m // lane_rows, put, 0, unroll=2)
-        half = pl.ds(first, ret.shape[0] // HALVES)
-        store(ret.at[half], ret_hbm.at[half])
+        turns = m // lane_rows // PARTS
+        for q in range(PARTS):
+            lax.fori_loop(q * turns, (q + 1) * turns, put, 0, unroll=turns)
+            done = pl.ds(first + q * turns * size, turns * size)
+            store(ret.at[done], ret_hbm.at[done])
     for copy in stores:
         copy.wait()
 
@@ -177,9 +180,9 @@
             scratch((CHUNKS, total // HALVES, part)),
             scratch((sources * block, part)),
             pltpu.SemaphoreType.DMA((3,)),
-            pltpu.SemaphoreType.DMA((PIECES,)),
-            pltpu.SemaphoreType.DMA((PIECES,)),
-            pltpu.SemaphoreType.DMA((3 + 3 * HALVES,)),
+            pltpu.SemaphoreType.DMA((HALVES,)),
+            pltpu.SemaphoreType.DMA((HALVES,)),
+            pltpu.SemaphoreType.DMA(((5 + PARTS) * HALVES,)),
         ],
         compiler_params=PARAMS,
         name="expert",
@@ -191,12 +194,6 @@
     tops, tok = probs.shape
     last = width - (CHUNKS - 1) * part
     mark = -(-last // 128) * 128
-
-    @pl.when(step == 0)
-    def _():
-        acc[...] = jnp.zeros_like(acc)
-        pacc[...] = jnp.zeros_like(pacc)
-
     hit = hits[...]
     own = hit[:tok]
     for k in range(1, tops):
@@ -204,17 +201,29 @@
     mask = masks[...]
     spread = jnp.concatenate([own * mask[c : c + 1] for c in range(CHUNKS)], axis=0)
     blk = back[...]
-    acc[...] += lax.dot_general(spread, blk, NN, preferred_element_type=F32)
-    pacc[...] += lax.dot_general(hit * mask[CHUNKS - 1 : CHUNKS], blk[:, mark : mark + 128], NN, preferred_element_type=F32)
+    total = lax.dot_general(spread, blk, NN, preferred_element_type=F32)
+    tails = hit * mask[CHUNKS - 1 : CHUNKS]
+    tails = lax.dot_general(tails, blk[:, mark : mark + 128], NN, preferred_element_type=F32)
+
+    @pl.when(step == 0)
+    def _():
+        acc[...] = total
+        pacc[...] = tails
+
+    @pl.when(step > 0)
+    def _():
+        acc[...] += total
+        pacc[...] += tails
 
     @pl.when(step == pl.num_programs(0) - 1)
     def _():
         for c in range(CHUNKS):
             w = min(part, width - c * part)
-            input_grad[c * part : c * part + w, :] = acc[c * tok : (c + 1) * tok, :].T[:w].astype(BF)
+            input_grad[c * part : c * part + w, :] = acc[c * tok : (c + 1) * tok, :].astype(BF).T[:w]
         for k in range(tops):
             col = pacc[k * tok : (k + 1) * tok, :].T
             prob_grad[k : k + 1, :] = (col[0:1] + col[1:2]) / probs[k : k + 1, :]
+
 
 def combine(back, hits, masks, probs_t, width):
     rows, part = back.shape
@@ -242,9 +251,10 @@
     return jnp.floor((x.astype(F32) + 0.5) * (1.0 / by)).astype(jnp.int32)
 
 
-def build_kernel(part, capacity, tokens_t, cotangent_t, position, probs, out, wide):
+def build_kernel(part, capacity, tokens_t, cotangent_t, ids, slots, probs, out, wide):
     width, tok = tokens_t.shape
-    tops = position.shape[0]
+    tops = ids.shape[0]
+    position = jnp.where(slots[...] >= 0, ids[...] * capacity + slots[...], -1)
 
     @pl.when(pl.program_id(0) == 0)
     def _():
@@ -278,22 +288,22 @@
         out[d, :, block:, :] = cot.reshape(experts, block, part)
 
 
-def build(tokens_t, cotangent_t, position, probs, capacity, experts, part, holders):
+def build(tokens_t, cotangent_t, ids, slots, probs, capacity, experts, part, holders):
     width, tok = tokens_t.shape
-    tops = position.shape[0]
+    tops = ids.shape[0]
     both = 2 * CHUNKS * capacity
-    steps = 4
+    steps = STEPS
     whole = lambda shape: pl.BlockSpec(shape, lambda i: (0,) * len(shape))
     return pl.pallas_call(
         functools.partial(build_kernel, part, capacity),
         grid=(steps,),
         out_shape=jax.ShapeDtypeStruct((holders, experts, both, part), BF),
-        in_specs=[whole((width, tok)), whole((width, tok)), whole((tops, tok)), whole((tops, tok))],
+        in_specs=[whole((width, tok))] * 2 + [whole((tops, tok))] * 3,
         out_specs=pl.BlockSpec((holders, experts // steps, both, part), lambda i: (0, i, 0, 0)),
         scratch_shapes=[pltpu.VMEM((2, CHUNKS * tok, part), BF)],
         compiler_params=PARAMS,
         name="build",
-    )(tokens_t, cotangent_t, position, probs)
+    )(tokens_t, cotangent_t, ids, slots, probs)
 
 
 def body(tokens, cotangent, expert_ids, slots, probs, w_gate, w_up, w_down):
@@ -325,10 +335,10 @@
     gate_w = w_gate[0].T
     up_w = w_up[0].T
     down_w = w_down[0].T
-    sent = build(tokens.T, cotangent.T, position, probs_t, capacity, experts, part, holders)
+    sent = build(tokens.T, cotangent.T, expert_ids.T, slots.T, probs_t, capacity, experts, part, holders)
     recv = exchange(sent.reshape(devices, 2 * block, part))
     hits = (position.reshape(top_count * tok_rows, 1) == row_slot[None, :]).astype(BF)
-    masks = (row_chunk[None, : send_rows // 4] == jnp.arange(CHUNKS)[:, None]).astype(BF)
+    masks = (row_chunk[None, : send_rows // TURNS] == jnp.arange(CHUNKS)[:, None]).astype(BF)
     ret, rows, weighted, hidden, gate_grad, up_grad = expert(recv, order, order_t, gate_w, up_w, down_w)
     back = exchange(ret.reshape(devices, block, part)).reshape(devices * block, part)
     with jax.named_scope("weight_grads"):

time: 245 us -> 239 us (0.976)
  Pallas kernels: 51.2 us -> 46.6 us
where the time goes in v4:
time: 239 us; the launch traced here: 237 us
  blocking collectives  122 us (51%)
  Pallas kernels  46.6 us (19%)
  waiting for transfers between devices  39.1 us (16%)
  matrix products  18.3 us (8%)
  starting transfers between devices  10.5 us (4%)
    all_to_all x1, blocking collectives, exchange(): lax.all_to_all(blocks, ('dp', 'expert'), split_axis=0, concat_axis=0, til...  122 us
    all_to_all x1, waiting for transfers between devices, exchange(): lax.all_to_all(blocks, ('dp', 'expert'), split_axis=0, concat_axis=0, til...  39.1 us
    pallas_call x1, Pallas kernels, expert(): pl.pallas_call(functools.partial(expert_kernel, part), out_shape=(like((s...  32.4 us
    all_to_all x1, starting transfers between devices, exchange(): lax.all_to_all(blocks, ('dp', 'expert'), split_axis=0, concat_axis=0, til...  10.5 us
    dot_general x1, matrix products, body(): lax.dot_general(rows, up_grad, TN, preferred_element_type=F32).astype(BF)  7.88 us
    pallas_call x1, Pallas kernels, build(): pl.pallas_call(functools.partial(build_kernel, part, capacity), grid=(ste...  7.39 us
    pallas_call x1, Pallas kernels, combine(): pl.pallas_call(functools.partial(combine_kernel, part, width), grid=(rows...  6.79 us
    dot_general x1, matrix products, body(): lax.dot_general(weighted, hidden, TN, preferred_element_type=F32).astype(BF)  5.23 us
  transfers between devices with their start and end apart: 1, of which 1 were waited for; matrix products, arithmetic and copies ran while one was open for 8% of the time, Pallas kernels for 0%

profile of v4, /device:TPU:1, one launch (start us, length us, event | category | flops | bytes accessed | tf_op | source)
XLA Modules:
  0.0 237.4 jit_solution(8506989564354224334)
XLA Ops:
  0.6 7.4 %build.1 = bf16[2,64,48,768]{3,2,1,0:T(8,128)(2,1)} custom-call(bf16[2880,128]{1,0:T(8,128)(2,1)} %bitcast.42, bf16[2880,128]{1,0:T(8,128)(2,1)} %bitcast.43, s32[4,128]{1,0:T(4,128)} %bitcast.44, s32[4,128]{1,0:T(4,128)} %bitcast.45, f32[4,128]{1,0:T(4,128)} %bitcast.35), custom_call_target="tpu_custom_call" | custom-call | tf_op jit(solution)/shard_map/build/pallas_call | solution.py:297
  8.0 121.7 %all_to_all.10.recv_hbm = bf16[128,48,768]{2,1,0:T(8,128)(2,1)} all-to-all(bf16[128,48,768]{2,1,0:T(8,128)(2,1)} %bitcast.37), channel_id=1, replica_groups=mesh['expert'=64,'dp'=2] {'dp','expert'}, dimensions={0} | all-to-all | bytes 18874368 | tf_op jit(solution)/shard_map/all_to_all | solution.py:333
  129.7 32.4 %expert.1 = (bf16[3072,768]{1,0:T(8,128)(2,1)}, bf16[768,2880]{1,0:T(8,128)(2,1)}, bf16[768,2880]{1,0:T(8,128)(2,1)}, bf16[768,720]{1,0:T(8,128)(2,1)}, bf16[768...) custom-call(bf16[128,48,768]{2,1,0:T(8,128)(2,1)} %all_to_all.10.recv_hbm, bf16[192,192]{1,0:T(8,128)(2,1)} %constant.45.clone.order, ...), custom_call_target="tpu_custom_call" | custom-call | tf_op jit(solution)/shard_map/expert/pallas_call | solution.py:155
  162.1 0.0 copy-start.1
  162.1 0.0 copy-start.2
  162.1 0.0 copy-start.5
  162.1 10.5 %all-to-all-start.1 = ((bf16[128,24,768]{2,1,0:T(8,128)(2,1)}), bf16[128,24,768]{2,1,0:T(8,128)(2,1)}, u32[]{:S(2)}, u32[]{:S(2)}) async-start(bf16[128,24,768]{2,1,0:T(8,128)(2,1)} %bitcast.38), calls=%async_computation.1 | async-start | bytes 9437184 | tf_op jit(solution)/shard_map/all_to_all | solution.py:333
  172.7 0.0 copy-done.1
  172.7 0.0 copy-done.2
  172.8 0.0 slice-start.2
  172.8 0.3 compare_convert_fusion.hits
  173.1 0.0 copy-done.5
  173.1 0.0 slice-start.3
  173.1 0.0 copy-start.4
  173.1 0.0 slice-start
  173.1 7.9 %fusion.1 = bf16[1,2880,720]{1,2,0:T(8,128)(2,1)} fusion(bf16[768,2880]{1,0:T(8,128)(2,1)} %get-tuple-element.16, bf16[768,720]{1,0:T(8,128)(2,1)S(1)} %copy-done.5), kind=kOutput, calls=%fused_computation.4 | convolution fusion | flops 3187123200 | bytes 9676800 | tf_op jit(solution)/shard_map/weight_grads/dot_general | solution.py:347
  181.0 0.0 slice-done.2
  181.0 0.0 slice-done.3
  181.0 0.0 copy-done.4
  181.0 0.0 slice-start.1
  181.0 0.0 copy-start.3
  181.1 5.2 %fusion = bf16[1,2880,720]{1,2,0:T(8,128)(2,1)} fusion(bf16[768,2880]{1,0:T(8,128)(2,1)S(1)} %bitcast.49, bf16[768,720]{1,0:T(8,128)(2,1)S(1)} %copy-done.4), kind=kOutput, calls=%fused_computation.3 | convolution fusion | flops 3187123200 | bytes 9676800 | tf_op jit(solution)/shard_map/weight_grads/dot_general | solution.py:346
  186.3 0.0 slice-done
  186.3 0.0 slice-done.1
  186.3 0.0 copy-done.3
  186.3 0.0 copy-start
  186.3 5.2 %fusion.2 = bf16[1,2880,720]{1,2,0:T(8,128)(2,1)} fusion(bf16[768,2880]{1,0:T(8,128)(2,1)S(1)} %bitcast.47, bf16[768,720]{1,0:T(8,128)(2,1)S(1)} %copy-done.3), kind=kOutput, calls=%fused_computation.5 | convolution fusion | flops 3187123200 | bytes 9676800 | tf_op jit(solution)/shard_map/weight_grads/dot_general | solution.py:345
  191.6 39.1 %all-to-all-done.1 = bf16[128,24,768]{2,1,0:T(8,128)(2,1)} async-done(((bf16[128,24,768]{2,1,0:T(8,128)(2,1)}), bf16[128,24,768]{2,1,0:T(8,128)(2,1)}, u32[]{:S(2)}, u32[]{:S(2)}) %all-to-all-start.1) | async-done | bytes 4718624 | tf_op jit(solution)/shard_map/all_to_all | solution.py:333
  230.6 0.0 copy-done
  230.6 6.8 %combine.1 = (bf16[2880,128]{1,0:T(8,128)(2,1)}, f32[4,128]{1,0:T(4,128)}) custom-call(bf16[3072,768]{1,0:T(8,128)(2,1)} %bitcast.13.back, bf16[512,1536]{1,0:T(8,128)(2,1)S(1)} %compare_convert_fusion.hits, bf16[4,1536]{1,0:T(4,128)(2,1)S(1)} %fusion.3.masks, f32[4,128]{1,0:T(4,128)S(1)} %bitcast.36), custom_call_target="tpu_custom_call" | custom-call | tf_op jit(solution)/shard_map/combine/combine/pallas_call | solution.py:234
  (6 shorter events, 0.0 us)
Async XLA Ops:
  162.1 10.6 %copy-start.1 = (s32[128,4]{0,1:T(4,128)S(1)}, s32[128,4]{0,1:T(4,128)}, u32[]{:S(2)}) copy-start(s32[128,4]{0,1:T(4,128)} %param.12) | copy-start | bytes 6148
  162.1 10.6 %copy-start.2 = (s32[128,4]{0,1:T(4,128)S(1)}, s32[128,4]{0,1:T(4,128)}, u32[]{:S(2)}) copy-start(s32[128,4]{0,1:T(4,128)} %param.13) | copy-start | bytes 6148
  162.1 11.0 %copy-start.5 = (bf16[768,720]{1,0:T(8,128)(2,1)S(1)}, bf16[768,720]{1,0:T(8,128)(2,1)}, u32[]{:S(2)}) copy-start(bf16[768,720]{1,0:T(8,128)(2,1)} %get-tuple-element.18) | copy-start | bytes 3317764
  162.1 68.5 %all-to-all-start.1 = ((bf16[128,24,768]{2,1,0:T(8,128)(2,1)}), bf16[128,24,768]{2,1,0:T(8,128)(2,1)}, u32[]{:S(2)}, u32[]{:S(2)}) async-start(bf16[128,24,768]{2,1,0:T(8,128)(2,1)} %bitcast.38), calls=%async_computation.1 | async-start | bytes 9437184 | tf_op jit(solution)/shard_map/all_to_all | solution.py:333
  172.8 8.3 %slice-start.2 = ((s8[4521984]{0:T(1024)(128)(4,1)}), s8[4194304]{0:T(1024)(128)(4,1)S(1)}, s32[]{:S(2)}) async-start(s8[4521984]{0:T(1024)(128)(4,1)} %bitcast.48), calls=%async_computation.4 | async-start | bytes 8388608
  173.1 7.9 %slice-start.3 = ((s8[4521984]{0:T(1024)(128)(4,1)}), s8[327680]{0:T(1024)(128)(4,1)S(1)}, s32[]{:S(2)}) async-start(s8[4521984]{0:T(1024)(128)(4,1)} %bitcast.48), calls=%async_computation.5 | async-start | bytes 655360
  173.1 7.9 %copy-start.4 = (bf16[768,720]{1,0:T(8,128)(2,1)S(1)}, bf16[768,720]{1,0:T(8,128)(2,1)}, u32[]{:S(2)}) copy-start(bf16[768,720]{1,0:T(8,128)(2,1)} %get-tuple-element.17) | copy-start | bytes 3317764
  173.1 13.2 %slice-start = ((s8[4521984]{0:T(1024)(128)(4,1)}), s8[4194304]{0:T(1024)(128)(4,1)S(1)}, s32[]{:S(2)}) async-start(s8[4521984]{0:T(1024)(128)(4,1)} %bitcast.46), calls=%async_computation.2 | async-start | bytes 8388608
  181.0 5.3 %slice-start.1 = ((s8[4521984]{0:T(1024)(128)(4,1)}), s8[327680]{0:T(1024)(128)(4,1)S(1)}, s32[]{:S(2)}) async-start(s8[4521984]{0:T(1024)(128)(4,1)} %bitcast.46), calls=%async_computation.3 | async-start | bytes 655360
  181.0 5.2 %copy-start.3 = (bf16[768,720]{1,0:T(8,128)(2,1)S(1)}, bf16[768,720]{1,0:T(8,128)(2,1)}, u32[]{:S(2)}) copy-start(bf16[768,720]{1,0:T(8,128)(2,1)} %get-tuple-element.20) | copy-start | bytes 3317764
  186.3 44.3 %copy-start = (f32[128,4]{0,1:T(4,128)S(1)}, f32[128,4]{0,1:T(4,128)}, u32[]{:S(2)}) copy-start(f32[128,4]{0,1:T(4,128)} %param.14) | copy-start | bytes 6148

commit v5 on v4

--- a/solution.py
+++ b/solution.py
@@ -138,7 +138,7 @@
 
         turns = m // lane_rows // PARTS
         for q in range(PARTS):
-            lax.fori_loop(q * turns, (q + 1) * turns, put, 0, unroll=turns)
+            lax.fori_loop(q * turns, (q + 1) * turns, put, 0, unroll=2)
             done = pl.ds(first + q * turns * size, turns * size)
             store(ret.at[done], ret_hbm.at[done])
     for copy in stores:

time: 239 us -> 238 us (level)
  no operation moved by 1% of the time
where the time goes in v5:
time: 238 us; the launch traced here: 236 us
  blocking collectives  122 us (51%)
  Pallas kernels  45.6 us (19%)
  waiting for transfers between devices  39.1 us (16%)
  matrix products  18.3 us (8%)
  starting transfers between devices  10.5 us (4%)
    all_to_all x1, blocking collectives, exchange(): lax.all_to_all(blocks, ('dp', 'expert'), split_axis=0, concat_axis=0, til...  122 us
    all_to_all x1, waiting for transfers between devices, exchange(): lax.all_to_all(blocks, ('dp', 'expert'), split_axis=0, concat_axis=0, til...  39.1 us
    pallas_call x1, Pallas kernels, expert(): pl.pallas_call(functools.partial(expert_kernel, part), out_shape=(like((s...  31.4 us
    all_to_all x1, starting transfers between devices, exchange(): lax.all_to_all(blocks, ('dp', 'expert'), split_axis=0, concat_axis=0, til...  10.5 us
    dot_general x1, matrix products, body(): lax.dot_general(rows, up_grad, TN, preferred_element_type=F32).astype(BF)  7.88 us
    pallas_call x1, Pallas kernels, build(): pl.pallas_call(functools.partial(build_kernel, part, capacity), grid=(ste...  7.39 us
    pallas_call x1, Pallas kernels, combine(): pl.pallas_call(functools.partial(combine_kernel, part, width), grid=(rows...  6.79 us
    dot_general x1, matrix products, body(): lax.dot_general(rows, gate_grad, TN, preferred_element_type=F32).astype(BF)  5.23 us
  transfers between devices with their start and end apart: 1, of which 1 were waited for; matrix products, arithmetic and copies ran while one was open for 8% of the time, Pallas kernels for 0%

profile of v5, /device:TPU:1, one launch (start us, length us, event | category | flops | bytes accessed | tf_op | source)
XLA Modules:
  0.0 236.4 jit_solution(9094151553834115599)
XLA Ops:
  0.6 7.4 %build.1 = bf16[2,64,48,768]{3,2,1,0:T(8,128)(2,1)} custom-call(bf16[2880,128]{1,0:T(8,128)(2,1)} %bitcast.42, bf16[2880,128]{1,0:T(8,128)(2,1)} %bitcast.43, s32[4,128]{1,0:T(4,128)} %bitcast.44, s32[4,128]{1,0:T(4,128)} %bitcast.45, f32[4,128]{1,0:T(4,128)} %bitcast.35), custom_call_target="tpu_custom_call" | custom-call | tf_op jit(solution)/shard_map/build/pallas_call | solution.py:297
  8.0 121.7 %all_to_all.10.recv_hbm = bf16[128,48,768]{2,1,0:T(8,128)(2,1)} all-to-all(bf16[128,48,768]{2,1,0:T(8,128)(2,1)} %bitcast.37), channel_id=1, replica_groups=mesh['expert'=64,'dp'=2] {'dp','expert'}, dimensions={0} | all-to-all | bytes 18874368 | tf_op jit(solution)/shard_map/all_to_all | solution.py:333
  129.7 31.4 %expert.1 = (bf16[3072,768]{1,0:T(8,128)(2,1)}, bf16[768,2880]{1,0:T(8,128)(2,1)}, bf16[768,2880]{1,0:T(8,128)(2,1)}, bf16[768,720]{1,0:T(8,128)(2,1)}, bf16[768...) custom-call(bf16[128,48,768]{2,1,0:T(8,128)(2,1)} %all_to_all.10.recv_hbm, bf16[192,192]{1,0:T(8,128)(2,1)} %constant.45.clone.order, ...), custom_call_target="tpu_custom_call" | custom-call | tf_op jit(solution)/shard_map/expert/pallas_call | solution.py:155
  161.1 0.0 copy-start.1
  161.1 0.0 copy-start.2
  161.1 0.0 copy-start.5
  161.1 10.5 %all-to-all-start.1 = ((bf16[128,24,768]{2,1,0:T(8,128)(2,1)}), bf16[128,24,768]{2,1,0:T(8,128)(2,1)}, u32[]{:S(2)}, u32[]{:S(2)}) async-start(bf16[128,24,768]{2,1,0:T(8,128)(2,1)} %bitcast.38), calls=%async_computation.1 | async-start | bytes 9437184 | tf_op jit(solution)/shard_map/all_to_all | solution.py:333
  171.7 0.0 copy-done.1
  171.7 0.0 copy-done.2
  171.7 0.0 slice-start.2
  171.7 0.3 compare_convert_fusion.hits
  172.1 0.0 copy-done.5
  172.1 0.0 slice-start.3
  172.1 0.0 copy-start.4
  172.1 0.0 slice-start
  172.1 7.9 %fusion.1 = bf16[1,2880,720]{1,2,0:T(8,128)(2,1)} fusion(bf16[768,2880]{1,0:T(8,128)(2,1)} %get-tuple-element.16, bf16[768,720]{1,0:T(8,128)(2,1)S(1)} %copy-done.5), kind=kOutput, calls=%fused_computation.4 | convolution fusion | flops 3187123200 | bytes 9676800 | tf_op jit(solution)/shard_map/weight_grads/dot_general | solution.py:347
  180.0 0.0 slice-done.2
  180.0 0.0 slice-done.3
  180.0 0.0 copy-done.4
  180.0 0.0 slice-start.1
  180.0 0.0 copy-start.3
  180.0 5.2 %fusion = bf16[1,2880,720]{1,2,0:T(8,128)(2,1)} fusion(bf16[768,2880]{1,0:T(8,128)(2,1)S(1)} %bitcast.49, bf16[768,720]{1,0:T(8,128)(2,1)S(1)} %copy-done.4), kind=kOutput, calls=%fused_computation.3 | convolution fusion | flops 3187123200 | bytes 9676800 | tf_op jit(solution)/shard_map/weight_grads/dot_general | solution.py:346
  185.3 0.0 slice-done
  185.3 0.0 slice-done.1
  185.3 0.0 copy-done.3
  185.3 0.0 copy-start
  185.3 5.2 %fusion.2 = bf16[1,2880,720]{1,2,0:T(8,128)(2,1)} fusion(bf16[768,2880]{1,0:T(8,128)(2,1)S(1)} %bitcast.47, bf16[768,720]{1,0:T(8,128)(2,1)S(1)} %copy-done.3), kind=kOutput, calls=%fused_computation.5 | convolution fusion | flops 3187123200 | bytes 9676800 | tf_op jit(solution)/shard_map/weight_grads/dot_general | solution.py:345
  190.5 39.1 %all-to-all-done.1 = bf16[128,24,768]{2,1,0:T(8,128)(2,1)} async-done(((bf16[128,24,768]{2,1,0:T(8,128)(2,1)}), bf16[128,24,768]{2,1,0:T(8,128)(2,1)}, u32[]{:S(2)}, u32[]{:S(2)}) %all-to-all-start.1) | async-done | bytes 4718624 | tf_op jit(solution)/shard_map/all_to_all | solution.py:333
  229.6 0.0 copy-done
  229.6 6.8 %combine.1 = (bf16[2880,128]{1,0:T(8,128)(2,1)}, f32[4,128]{1,0:T(4,128)}) custom-call(bf16[3072,768]{1,0:T(8,128)(2,1)} %bitcast.13.back, bf16[512,1536]{1,0:T(8,128)(2,1)S(1)} %compare_convert_fusion.hits, bf16[4,1536]{1,0:T(4,128)(2,1)S(1)} %fusion.3.masks, f32[4,128]{1,0:T(4,128)S(1)} %bitcast.36), custom_call_target="tpu_custom_call" | custom-call | tf_op jit(solution)/shard_map/combine/combine/pallas_call | solution.py:234
  (6 shorter events, 0.0 us)
Async XLA Ops:
  161.1 10.6 %copy-start.1 = (s32[128,4]{0,1:T(4,128)S(1)}, s32[128,4]{0,1:T(4,128)}, u32[]{:S(2)}) copy-start(s32[128,4]{0,1:T(4,128)} %param.12) | copy-start | bytes 6148
  161.1 10.6 %copy-start.2 = (s32[128,4]{0,1:T(4,128)S(1)}, s32[128,4]{0,1:T(4,128)}, u32[]{:S(2)}) copy-start(s32[128,4]{0,1:T(4,128)} %param.13) | copy-start | bytes 6148
  161.1 11.0 %copy-start.5 = (bf16[768,720]{1,0:T(8,128)(2,1)S(1)}, bf16[768,720]{1,0:T(8,128)(2,1)}, u32[]{:S(2)}) copy-start(bf16[768,720]{1,0:T(8,128)(2,1)} %get-tuple-element.18) | copy-start | bytes 3317764
  161.1 68.5 %all-to-all-start.1 = ((bf16[128,24,768]{2,1,0:T(8,128)(2,1)}), bf16[128,24,768]{2,1,0:T(8,128)(2,1)}, u32[]{:S(2)}, u32[]{:S(2)}) async-start(bf16[128,24,768]{2,1,0:T(8,128)(2,1)} %bitcast.38), calls=%async_computation.1 | async-start | bytes 9437184 | tf_op jit(solution)/shard_map/all_to_all | solution.py:333
  171.7 8.3 %slice-start.2 = ((s8[4521984]{0:T(1024)(128)(4,1)}), s8[4194304]{0:T(1024)(128)(4,1)S(1)}, s32[]{:S(2)}) async-start(s8[4521984]{0:T(1024)(128)(4,1)} %bitcast.48), calls=%async_computation.4 | async-start | bytes 8388608
  172.1 7.9 %slice-start.3 = ((s8[4521984]{0:T(1024)(128)(4,1)}), s8[327680]{0:T(1024)(128)(4,1)S(1)}, s32[]{:S(2)}) async-start(s8[4521984]{0:T(1024)(128)(4,1)} %bitcast.48), calls=%async_computation.5 | async-start | bytes 655360
  172.1 7.9 %copy-start.4 = (bf16[768,720]{1,0:T(8,128)(2,1)S(1)}, bf16[768,720]{1,0:T(8,128)(2,1)}, u32[]{:S(2)}) copy-start(bf16[768,720]{1,0:T(8,128)(2,1)} %get-tuple-element.17) | copy-start | bytes 3317764
  172.1 13.2 %slice-start = ((s8[4521984]{0:T(1024)(128)(4,1)}), s8[4194304]{0:T(1024)(128)(4,1)S(1)}, s32[]{:S(2)}) async-start(s8[4521984]{0:T(1024)(128)(4,1)} %bitcast.46), calls=%async_computation.2 | async-start | bytes 8388608
  180.0 5.3 %slice-start.1 = ((s8[4521984]{0:T(1024)(128)(4,1)}), s8[327680]{0:T(1024)(128)(4,1)S(1)}, s32[]{:S(2)}) async-start(s8[4521984]{0:T(1024)(128)(4,1)} %bitcast.46), calls=%async_computation.3 | async-start | bytes 655360
  180.0 5.3 %copy-start.3 = (bf16[768,720]{1,0:T(8,128)(2,1)S(1)}, bf16[768,720]{1,0:T(8,128)(2,1)}, u32[]{:S(2)}) copy-start(bf16[768,720]{1,0:T(8,128)(2,1)} %get-tuple-element.20) | copy-start | bytes 3317764
  185.3 44.3 %copy-start = (f32[128,4]{0,1:T(4,128)S(1)}, f32[128,4]{0,1:T(4,128)}, u32[]{:S(2)}) copy-start(f32[128,4]{0,1:T(4,128)} %param.14) | copy-start | bytes 6148
